TPU v7x, 32 devices: a whole 2x2x4 slice. The times are simulated.
32 devices in a mesh: row: 4 (over x, core), theta: 4 (over z), phi: 2 (over y).
Axes of the slice: x: 2, y: 2, z: 4, core: 2. Of those that a mesh axis runs over, the one named last changes fastest.
Arguments:
- magnetic: float32 [3, 48, 64, 256], P(None, 'row', 'theta', 'phi'), may hold values from -6 to 6
- electric: float32 [3, 48, 64, 256], P(None, 'row', 'theta', 'phi'), may hold values from -6 to 6
Outputs:
- magnetic_new: float32 [3, 48, 64, 256], P(None, 'row', 'theta', 'phi')
- electric_new: float32 [3, 48, 64, 256], P(None, 'row', 'theta', 'phi')
All inputs are finite; a program needn't handle non-finite values.
Results may differ from a plain program's by a relative error of at most 0.0001.
Values sent between devices are 32-bit elements; how exact they have to be, the bound alone decides.
No kernel may reach another device: no remote copies, remote signals or barrier semaphores. Data moves between devices by JAX's collectives and lax.ppermute only.
A program may use at most 64 MiB of HBM per device.

v0:
```python
import math

import jax
import jax.numpy as jnp
from jax import lax
from jax.sharding import PartitionSpec as P

hole_mass = 1.0
inner_radius = 1.8
wave_speed = 1.25
courant = 0.3
smooth_eps = 1e-06


def padded_2(block, sides, width, periodic):
    for axis, dim in sides:
        count = lax.axis_size(axis)
        forward = [(i, i + 1) for i in range(count - 1)]
        if periodic:
            forward.append((count - 1, 0))
        backward = [(target, source) for source, target in forward]
        low = lax.ppermute(
            lax.slice_in_dim(block, block.shape[dim] - width, None, axis=dim), axis, forward
        )
        high = lax.ppermute(lax.slice_in_dim(block, 0, width, axis=dim), axis, backward)
        block = jnp.concatenate([low, block, high], axis=dim)
    return block


def from_behind(array, axis, by):
    length = lax.axis_size(axis)
    return lax.ppermute(array, axis, [(i, (i + by) % length) for i in range(length)])


def weno_face(far_left, near_left, center, near_right, far_right):
    cand_low = (2.0 * far_left - 7.0 * near_left + 11.0 * center) / 6.0
    cand_mid = (-near_left + 5.0 * center + 2.0 * near_right) / 6.0
    cand_high = (2.0 * center + 5.0 * near_right - far_right) / 6.0
    rough_low = (
        13.0 / 12.0 * (far_left - 2.0 * near_left + center) ** 2
        + 0.25 * (far_left - 4.0 * near_left + 3.0 * center) ** 2
    )
    rough_mid = (
        13.0 / 12.0 * (near_left - 2.0 * center + near_right) ** 2
        + 0.25 * (near_left - near_right) ** 2
    )
    rough_high = (
        13.0 / 12.0 * (center - 2.0 * near_right + far_right) ** 2
        + 0.25 * (3.0 * center - 4.0 * near_right + far_right) ** 2
    )
    alpha_low = 0.1 / (smooth_eps + rough_low) ** 2
    alpha_mid = 0.6 / (smooth_eps + rough_mid) ** 2
    alpha_high = 0.3 / (smooth_eps + rough_high) ** 2
    return (alpha_low * cand_low + alpha_mid * cand_mid + alpha_high * cand_high) / (
        alpha_low + alpha_mid + alpha_high
    )


def interface(flux, field, axis):
    faces = flux.shape[axis] - 5
    plus_part = 0.5 * (flux + wave_speed * field)
    minus_part = 0.5 * (flux - wave_speed * field)
    plus_cuts = [
        lax.slice_in_dim(plus_part, offset, offset + faces, axis=axis) for offset in range(6)
    ]
    minus_cuts = [
        lax.slice_in_dim(minus_part, offset, offset + faces, axis=axis) for offset in range(6)
    ]
    left_state = weno_face(plus_cuts[0], plus_cuts[1], plus_cuts[2], plus_cuts[3], plus_cuts[4])
    right_state = weno_face(
        minus_cuts[5], minus_cuts[4], minus_cuts[3], minus_cuts[2], minus_cuts[1]
    )
    return left_state + right_state


def face_fluxes(fluxes, fields, axis):
    return lax.map(lambda couple: interface(couple[0], couple[1], axis), (fluxes, fields))


def tendency(padded, radii, angles, spacing_r, spacing_theta, spacing_phi):
    ratio = 2.0 * hole_mass / radii
    lapse_factor = (1.0 / jnp.sqrt(1.0 + ratio))[:, None, None]
    shift_speed = (ratio / (1.0 + ratio))[:, None, None]
    b_radial, b_polar, b_azimuth = (padded[0], padded[1], padded[2])
    d_radial, d_polar, d_azimuth = (padded[3], padded[4], padded[5])
    e_radial = lapse_factor * d_radial
    e_polar = lapse_factor * d_polar - shift_speed * b_azimuth
    e_azimuth = lapse_factor * d_azimuth + shift_speed * b_polar
    h_radial = lapse_factor * b_radial
    h_polar = lapse_factor * b_polar + shift_speed * d_azimuth
    h_azimuth = lapse_factor * b_azimuth - shift_speed * d_polar
    zeros_field = jnp.zeros_like(b_radial)
    radial_flux = jnp.stack([zeros_field, -e_azimuth, e_polar, zeros_field, h_azimuth, -h_polar])
    polar_flux = jnp.stack([e_azimuth, zeros_field, -e_radial, -h_azimuth, zeros_field, h_radial])
    azimuth_flux = jnp.stack([-e_polar, e_radial, zeros_field, h_polar, -h_radial, zeros_field])
    radial_faces = face_fluxes(radial_flux[:, :, 3:-3, 3:-3], padded[:, :, 3:-3, 3:-3], 0)
    polar_faces = face_fluxes(polar_flux[:, 3:-3, :, 3:-3], padded[:, 3:-3, :, 3:-3], 1)
    azimuth_faces = face_fluxes(azimuth_flux[:, 3:-3, 3:-3, :], padded[:, 3:-3, 3:-3, :], 2)
    radius_face = (0.5 * (radii[2:-3] + radii[3:-2])) ** 2
    radius_cell = radii[3:-3] ** 2
    sine_face = jnp.sin(0.5 * (angles[2:-3] + angles[3:-2]))
    sine_cell = jnp.sin(angles[3:-3])
    radial_div = (
        radius_face[None, 1:, None, None] * radial_faces[:, 1:]
        - radius_face[None, :-1, None, None] * radial_faces[:, :-1]
    ) / (radius_cell[None, :, None, None] * spacing_r)
    polar_div = (
        sine_face[None, None, 1:, None] * polar_faces[:, :, 1:]
        - sine_face[None, None, :-1, None] * polar_faces[:, :, :-1]
    ) / (sine_cell[None, None, :, None] * spacing_theta)
    azimuth_div = (azimuth_faces[:, :, :, 1:] - azimuth_faces[:, :, :, :-1]) / spacing_phi
    return -(radial_div + polar_div + azimuth_div)


def project(fields):
    magnetic_part = fields[:3]
    electric_part = fields[3:]
    b_square = jnp.maximum(jnp.sum(magnetic_part * magnetic_part, axis=0), 1.0)
    along = jnp.sum(magnetic_part * electric_part, axis=0) / b_square
    electric_part = electric_part - along[None] * magnetic_part
    d_square = jnp.sum(electric_part * electric_part, axis=0)
    shrink = jnp.sqrt(b_square / jnp.maximum(d_square, b_square))
    return jnp.concatenate([magnetic_part, electric_part * shrink[None]], axis=0)


def body(magnetic, electric):
    fields = jnp.concatenate([magnetic, electric], axis=0)
    rows_dev = fields.shape[1]
    theta_dev = fields.shape[2]
    n_theta = lax.axis_size("theta")
    n_phi = lax.axis_size("phi")
    n_row = lax.axis_size("row")
    total_rows = rows_dev * n_row
    spacing_theta = math.pi / (theta_dev * n_theta)
    spacing_phi = 2.0 * math.pi / (fields.shape[3] * n_phi)
    step_dt = courant / (1.0 / spacing_theta + 1.0 / spacing_theta + 1.0 / spacing_phi)
    row_start = lax.axis_index("row") * rows_dev
    theta_index = lax.axis_index("theta")
    angles = (
        (theta_index * theta_dev - 3 + jnp.arange(theta_dev + 6)).astype(jnp.float32) + 0.5
    ) * spacing_theta
    parity = jnp.array([1.0, -1.0, -1.0, 1.0, -1.0, -1.0], jnp.float32)[:, None, None, None]
    weights = (0.0, 0.75, 1.0 / 3.0)
    current = fields
    for section_index in range(3):
        extended = padded_2(current, (("phi", 3),), 3, True)
        extended = padded_2(extended, (("row", 1),), 3, False)
        polar_padded = padded_2(extended, (("theta", 2),), 3, False)
        north_rows = polar_padded[:, :, 5:2:-1, :]
        south_rows = polar_padded[:, :, -4:-7:-1, :]
        outgoing = jnp.where(theta_index == 0, north_rows, south_rows)
        incoming = from_behind(outgoing, "phi", n_phi // 2)
        upper_ghost = jnp.where(theta_index == 0, incoming * parity, polar_padded[:, :, :3])
        lower_ghost = jnp.where(
            theta_index == n_theta - 1, incoming * parity, polar_padded[:, :, -3:]
        )
        weight = weights[section_index]
        global_rows = row_start - 3 + jnp.arange(rows_dev + 2 * 3)
        radii = inner_radius + (global_rows.astype(jnp.float32) + 0.5) * spacing_theta
        rates = tendency(
            jnp.concatenate([upper_ghost, polar_padded[:, :, 3:-3], lower_ghost], axis=2),
            radii,
            angles,
            spacing_theta,
            spacing_theta,
            spacing_phi,
        )
        updated = project(weight * fields + (1.0 - weight) * (current + step_dt * rates))
        kept_rows = global_rows[3:-3]
        inside = (kept_rows >= 0) & (kept_rows < total_rows)
        current = jnp.where(inside[None, :, None, None], updated, 0.0)
    return (current[:3], current[3:])


def solution(mesh):
    in_specs = (P(None, "row", "theta", "phi"), P(None, "row", "theta", "phi"))
    out_specs = (P(None, "row", "theta", "phi"), P(None, "row", "theta", "phi"))
    return jax.shard_map(body, mesh=mesh, in_specs=in_specs, out_specs=out_specs, check_vma=False)
```

profile of v0, /device:TPU:1, one launch (start us, length us, event | category | flops | bytes accessed | tf_op | source)
XLA Modules:
  0.0 315.9 jit_solution(1438143854139053936)
XLA Ops:
  3.5 2.1 collective-permute-start
  9.7 2.7 collective-permute-done.1
  14.2 4.5 %collective-permute-start.2 = (f32[6,3,16,134]{3,2,1,0:T(8,128)}, f32[6,3,16,134]{3,2,1,0:T(8,128)S(1)}, u32[]{:S(2)}, u32[]{:S(2)}) collective-permute-start(f32[6,3,16,134]{3,2,1,0:T(8,128)} %get-tuple-element.387), channel_id=1, source_target_pairs={{0,8},{8,16},{16,24},{1,9},{9,17},{17,25},{2,10},{10,18},{18,26},{... | collective-permute-start | bytes 463112 | tf_op jit(solution)/shard_map/ppermute | solution.py:22
  18.7 1.9 collective-permute-start.3
  22.6 4.3 %collective-permute-done.3 = f32[6,3,16,134]{3,2,1,0:T(8,128)S(1)} collective-permute-done((f32[6,3,16,134]{3,2,1,0:T(8,128)}, f32[6,3,16,134]{3,2,1,0:T(8,128)S(1)}, u32[]{:S(2)}, u32[]{:S(2)}) %collective-permute-start.3) | collective-permute-done | bytes 154400 | tf_op jit(solution)/shard_map/ppermute | solution.py:25
  29.2 4.0 %collective-permute-start.5 = (f32[6,18,3,134]{3,1,2,0:T(8,128)}, f32[6,18,3,134]{3,1,2,0:T(8,128)}, u32[]{:S(2)}, u32[]{:S(2)}) collective-permute-start(f32[6,18,3,134]{3,1,2,0:T(8,128)} %copy.242), channel_id=1, source_target_pairs={{0,2},{2,4},{4,6},{1,3},{3,5},{5,7},{8,10},{10,12},{12,14},{9,11},... | collective-permute-start | bytes 521000 | tf_op jit(solution)/shard_map/ppermute | solution.py:22
  34.6 2.0 reverse_select_fusion.2
  39.0 5.9 %collective-permute-done.4 = f32[6,18,3,134]{3,1,2,0:T(8,128)} collective-permute-done((f32[6,18,3,134]{3,1,2,0:T(8,128)}, f32[6,18,3,134]{3,1,2,0:T(8,128)}, u32[]{:S(2)}, u32[]{:S(2)}) %collective-permute-start.4) | collective-permute-done | bytes 173696 | tf_op jit(solution)/shard_map/ppermute | solution.py:32
  53.0 8.3 %while.90 = (s32[]{:T(128)}, f32[6,13,16,128]{3,2,1,0:T(8,128)S(1)}, f32[6,18,16,128]{3,2,1,0:T(8,128)S(1)}, f32[6,18,16,128]{3,2,1,0:T(8,128)}, s32[]{:T(128)}) while((s32[]{:T(128)}, f32[6,13,16,128]{3,2,1,0:T(8,128)S(1)}, f32[6,18,16,128]{3,2,1,0:T(8,128)S(1)}, f32[6,18,16,128]{3,2,1,0:T(8,128)}, s32[]{:T(128)}) %tuple.213), condition=%wide.region_1.2_spmd, body=%wide.region_0.1_spmd.sunk | while | flops 3618818 | bytes 1761349 | solution.py:77
  62.2 2.1 fusion.1
  64.4 2.7 slice.841
  67.2 10.7 %while.91 = (s32[]{:T(128)}, f32[6,12,17,128]{3,2,1,0:T(8,128)S(1)}, f32[6,12,22,128]{3,2,1,0:T(8,128)}, f32[6,12,22,128]{3,2,1,0:T(8,128)}, s32[]{:T(128)}) while((s32[]{:T(128)}, f32[6,12,17,128]{3,2,1,0:T(8,128)S(1)}, f32[6,12,22,128]{3,2,1,0:T(8,128)}, f32[6,12,22,128]{3,2,1,0:T(8,128)}, s32[]{:T(128)}) %tuple.210), condition=%wide.region_3.4_spmd, body=%wide.region_2.3_spmd.sunk | while | flops 3537410 | bytes 2162757 | solution.py:77
  78.7 2.7 slice.843
  82.6 16.1 %while.92 = (s32[]{:T(128)}, f32[6,12,16,129]{3,2,1,0:T(8,128)}, f32[6,12,16,134]{3,2,1,0:T(8,128)}, f32[6,12,16,134]{3,2,1,0:T(8,128)S(1)}, s32[]{:T(128)}) while((s32[]{:T(128)}, f32[6,12,16,129]{3,2,1,0:T(8,128)}, f32[6,12,16,134]{3,2,1,0:T(8,128)}, f32[6,12,16,134]{3,2,1,0:T(8,128)S(1)}, s32[]{:T(128)}) %tuple.207), condition=%wide.region_5.6_spmd, body=%wide.region_4.5_spmd.sunk | while | flops 3323714 | bytes 1599553 | solution.py:77
  89.0 1.7 bitcast_dynamic-update-slice_fusion.20
  98.7 1.9 add_add_fusion
  104.5 3.0 collective-permute-done.7
  110.1 1.9 collective-permute-start.10
  112.0 3.6 %collective-permute-start.9 = (f32[6,3,16,134]{3,2,1,0:T(8,128)S(1)}, f32[6,3,16,134]{3,2,1,0:T(8,128)S(1)}, u32[]{:S(2)}, u32[]{:S(2)}) collective-permute-start(f32[6,3,16,134]{3,2,1,0:T(8,128)S(1)} %get-tuple-element.385), channel_id=1, source_target_pairs={{0,8},{8,16},{16,24},{1,9},{9,17},{17,25},{2,10},{10,18},{18,26},{... | collective-permute-start | bytes 463112 | tf_op jit(solution)/shard_map/ppermute | solution.py:22
  115.7 2.5 collective-permute-done.10
  121.6 5.4 %collective-permute-start.12 = (f32[6,18,3,134]{3,1,2,0:T(8,128)}, f32[6,18,3,134]{3,1,2,0:T(8,128)}, u32[]{:S(2)}, u32[]{:S(2)}) collective-permute-start(f32[6,18,3,134]{3,1,2,0:T(8,128)} %copy.244), channel_id=1, source_target_pairs={{0,2},{2,4},{4,6},{1,3},{3,5},{5,7},{8,10},{10,12},{12,14},{9,11},... | collective-permute-start | bytes 521000 | tf_op jit(solution)/shard_map/ppermute | solution.py:22
  127.0 2.0 reverse_select_fusion.1
  131.9 2.3 pad_maximum_fusion.10
  134.2 5.6 %collective-permute-done.11 = f32[6,18,3,134]{3,1,2,0:T(8,128)} collective-permute-done((f32[6,18,3,134]{3,1,2,0:T(8,128)}, f32[6,18,3,134]{3,1,2,0:T(8,128)}, u32[]{:S(2)}, u32[]{:S(2)}) %collective-permute-start.11) | collective-permute-done | bytes 173696 | tf_op jit(solution)/shard_map/ppermute | solution.py:32
  149.3 12.5 %while.93 = (s32[]{:T(128)}, f32[6,13,16,128]{3,2,1,0:T(8,128)}, f32[6,18,16,128]{3,2,1,0:T(8,128)}, f32[6,18,16,128]{3,2,1,0:T(8,128)}, s32[]{:T(128)}) while((s32[]{:T(128)}, f32[6,13,16,128]{3,2,1,0:T(8,128)}, f32[6,18,16,128]{3,2,1,0:T(8,128)}, f32[6,18,16,128]{3,2,1,0:T(8,128)}, s32[]{:T(128)}) %tuple.222), condition=%wide.region_10.11_spmd, body=%wide.region_9.10_spmd.sunk | while | flops 3618818 | bytes 1761857 | solution.py:77
  162.7 2.1 fusion.3
  164.8 2.7 slice.857
  168.5 14.6 %while.94 = (s32[]{:T(128)}, f32[6,12,17,128]{3,2,1,0:T(8,128)}, f32[6,12,22,128]{3,2,1,0:T(8,128)}, f32[6,12,22,128]{3,2,1,0:T(8,128)}, s32[]{:T(128)}) while((s32[]{:T(128)}, f32[6,12,17,128]{3,2,1,0:T(8,128)}, f32[6,12,22,128]{3,2,1,0:T(8,128)}, f32[6,12,22,128]{3,2,1,0:T(8,128)}, s32[]{:T(128)}) %tuple.219), condition=%wide.region_12.13_spmd, body=%wide.region_11.12_spmd.sunk | while | flops 3537410 | bytes 1733185 | solution.py:77
  183.9 2.7 slice.859
  187.8 16.1 %while.95 = (s32[]{:T(128)}, f32[6,12,16,129]{3,2,1,0:T(8,128)}, f32[6,12,16,134]{3,2,1,0:T(8,128)}, f32[6,12,16,134]{3,2,1,0:T(8,128)S(1)}, s32[]{:T(128)}) while((s32[]{:T(128)}, f32[6,12,16,129]{3,2,1,0:T(8,128)}, f32[6,12,16,134]{3,2,1,0:T(8,128)}, f32[6,12,16,134]{3,2,1,0:T(8,128)S(1)}, s32[]{:T(128)}) %tuple.216), condition=%wide.region_14.15_spmd, body=%wide.region_13.14_spmd.sunk | while | flops 3323714 | bytes 1599553 | solution.py:77
  194.2 1.7 bitcast_dynamic-update-slice_fusion.23
  203.9 2.8 multiply_add_fusion.1
  210.6 3.2 %collective-permute-done.14 = f32[6,12,16,3]{2,1,3,0:T(8,128)S(1)} collective-permute-done((f32[6,12,16,3]{2,1,3,0:T(8,128)S(1)}, f32[6,12,16,3]{2,1,3,0:T(8,128)S(1)}, u32[]{:S(2)}, u32[]{:S(2)}) %collective-permute-start.14) | collective-permute-done | bytes 13856 | tf_op jit(solution)/shard_map/ppermute | solution.py:22
  216.5 3.8 %collective-permute-start.16 = (f32[6,3,16,134]{3,2,1,0:T(8,128)S(1)}, f32[6,3,16,134]{3,2,1,0:T(8,128)S(1)}, u32[]{:S(2)}, u32[]{:S(2)}) collective-permute-start(f32[6,3,16,134]{3,2,1,0:T(8,128)S(1)} %get-tuple-element.383), channel_id=1, source_target_pairs={{0,8},{8,16},{16,24},{1,9},{9,17},{17,25},{2,10},{10,18},{18,26},{... | collective-permute-start | bytes 463112 | tf_op jit(solution)/shard_map/ppermute | solution.py:22
  220.3 1.9 collective-permute-start.17
  222.2 1.7 collective-permute-done.16
  223.9 4.4 %collective-permute-done.17 = f32[6,3,16,134]{3,2,1,0:T(8,128)S(1)} collective-permute-done((f32[6,3,16,134]{3,2,1,0:T(8,128)S(1)}, f32[6,3,16,134]{3,2,1,0:T(8,128)S(1)}, u32[]{:S(2)}, u32[]{:S(2)}) %collective-permute-start.17) | collective-permute-done | bytes 154400 | tf_op jit(solution)/shard_map/ppermute | solution.py:25
  230.5 4.9 %collective-permute-start.19 = (f32[6,18,3,134]{3,1,2,0:T(8,128)}, f32[6,18,3,134]{3,1,2,0:T(8,128)}, u32[]{:S(2)}, u32[]{:S(2)}) collective-permute-start(f32[6,18,3,134]{3,1,2,0:T(8,128)} %copy.246), channel_id=1, source_target_pairs={{0,2},{2,4},{4,6},{1,3},{3,5},{5,7},{8,10},{10,12},{12,14},{9,11},... | collective-permute-start | bytes 521000 | tf_op jit(solution)/shard_map/ppermute | solution.py:22
  235.4 2.0 reverse_select_fusion
  240.7 2.3 pad_maximum_fusion.6
  242.9 4.4 %collective-permute-done.18 = f32[6,18,3,134]{3,1,2,0:T(8,128)} collective-permute-done((f32[6,18,3,134]{3,1,2,0:T(8,128)}, f32[6,18,3,134]{3,1,2,0:T(8,128)}, u32[]{:S(2)}, u32[]{:S(2)}) %collective-permute-start.18) | collective-permute-done | bytes 173696 | tf_op jit(solution)/shard_map/ppermute | solution.py:32
  256.8 12.5 %while.96 = (s32[]{:T(128)}, f32[6,13,16,128]{3,2,1,0:T(8,128)}, f32[6,18,16,128]{3,2,1,0:T(8,128)}, f32[6,18,16,128]{3,2,1,0:T(8,128)}, s32[]{:T(128)}) while((s32[]{:T(128)}, f32[6,13,16,128]{3,2,1,0:T(8,128)}, f32[6,18,16,128]{3,2,1,0:T(8,128)}, f32[6,18,16,128]{3,2,1,0:T(8,128)}, s32[]{:T(128)}) %tuple.231), condition=%wide.region_19.20_spmd, body=%wide.region_18.19_spmd.sunk | while | flops 3618818 | bytes 1761857 | solution.py:77
  270.2 2.1 fusion.5
  272.3 2.7 slice.873
  276.0 14.6 %while.97 = (s32[]{:T(128)}, f32[6,12,17,128]{3,2,1,0:T(8,128)}, f32[6,12,22,128]{3,2,1,0:T(8,128)}, f32[6,12,22,128]{3,2,1,0:T(8,128)}, s32[]{:T(128)}) while((s32[]{:T(128)}, f32[6,12,17,128]{3,2,1,0:T(8,128)}, f32[6,12,22,128]{3,2,1,0:T(8,128)}, f32[6,12,22,128]{3,2,1,0:T(8,128)}, s32[]{:T(128)}) %tuple.228), condition=%wide.region_21.22_spmd, body=%wide.region_20.21_spmd.sunk | while | flops 3537410 | bytes 1733185 | solution.py:77
  291.4 2.7 slice.875
  295.3 16.1 %while.98 = (s32[]{:T(128)}, f32[6,12,16,129]{3,2,1,0:T(8,128)}, f32[6,12,16,134]{3,2,1,0:T(8,128)}, f32[6,12,16,134]{3,2,1,0:T(8,128)S(1)}, s32[]{:T(128)}) while((s32[]{:T(128)}, f32[6,12,16,129]{3,2,1,0:T(8,128)}, f32[6,12,16,134]{3,2,1,0:T(8,128)}, f32[6,12,16,134]{3,2,1,0:T(8,128)S(1)}, s32[]{:T(128)}) %tuple.225), condition=%wide.region_23.24_spmd, body=%wide.region_22.23_spmd.sunk | while | flops 3323714 | bytes 1599553 | solution.py:77
  311.4 2.8 multiply_add_fusion
  (319 shorter events, 198.1 us)
Async XLA Ops:
  3.5 5.7 %collective-permute-start = (f32[6,12,16,3]{2,1,3,0:T(8,128)S(1)}, f32[6,12,16,3]{2,1,3,0:T(8,128)S(1)}, u32[]{:S(2)}, u32[]{:S(2)}) collective-permute-start(f32[6,12,16,3]{2,1,3,0:T(8,128)S(1)} %copy.239), channel_id=1, source_target_pairs={{0,1},{1,0},{2,3},{3,2},{4,5},{5,4},{6,7},{7,6},{8,9},{9,8},{10,11... | collective-permute-start | bytes 41480 | tf_op jit(solution)/shard_map/ppermute | solution.py:22
  6.3 6.0 %collective-permute-start.1 = (f32[6,12,16,3]{2,1,3,0:T(8,128)S(1)}, f32[6,12,16,3]{2,1,3,0:T(8,128)S(1)}, u32[]{:S(2)}, u32[]{:S(2)}) collective-permute-start(f32[6,12,16,3]{2,1,3,0:T(8,128)S(1)} %copy.240), channel_id=1, source_target_pairs={{1,0},{0,1},{3,2},{2,3},{5,4},{4,5},{7,6},{6,7},{9,8},{8,9},{11,10... | collective-permute-start | bytes 41480 | tf_op jit(solution)/shard_map/ppermute | solution.py:25
  14.2 8.4 %collective-permute-start.2 = (f32[6,3,16,134]{3,2,1,0:T(8,128)}, f32[6,3,16,134]{3,2,1,0:T(8,128)S(1)}, u32[]{:S(2)}, u32[]{:S(2)}) collective-permute-start(f32[6,3,16,134]{3,2,1,0:T(8,128)} %get-tuple-element.387), channel_id=1, source_target_pairs={{0,8},{8,16},{16,24},{1,9},{9,17},{17,25},{2,10},{10,18},{18,26},{... | collective-permute-start | bytes 463112 | tf_op jit(solution)/shard_map/ppermute | solution.py:22
  18.7 8.3 %collective-permute-start.3 = (f32[6,3,16,134]{3,2,1,0:T(8,128)}, f32[6,3,16,134]{3,2,1,0:T(8,128)S(1)}, u32[]{:S(2)}, u32[]{:S(2)}) collective-permute-start(f32[6,3,16,134]{3,2,1,0:T(8,128)} %get-tuple-element.388), channel_id=1, source_target_pairs={{8,0},{16,8},{24,16},{9,1},{17,9},{25,17},{10,2},{18,10},{26,18},{... | collective-permute-start | bytes 463112 | tf_op jit(solution)/shard_map/ppermute | solution.py:25
  29.2 15.8 %collective-permute-start.5 = (f32[6,18,3,134]{3,1,2,0:T(8,128)}, f32[6,18,3,134]{3,1,2,0:T(8,128)}, u32[]{:S(2)}, u32[]{:S(2)}) collective-permute-start(f32[6,18,3,134]{3,1,2,0:T(8,128)} %copy.242), channel_id=1, source_target_pairs={{0,2},{2,4},{4,6},{1,3},{3,5},{5,7},{8,10},{10,12},{12,14},{9,11},... | collective-permute-start | bytes 521000 | tf_op jit(solution)/shard_map/ppermute | solution.py:22
  33.1 11.8 %collective-permute-start.6 = (f32[6,18,3,134]{3,1,2,0:T(8,128)}, f32[6,18,3,134]{3,1,2,0:T(8,128)}, u32[]{:S(2)}, u32[]{:S(2)}) collective-permute-start(f32[6,18,3,134]{3,1,2,0:T(8,128)} %copy.241), channel_id=1, source_target_pairs={{2,0},{4,2},{6,4},{3,1},{5,3},{7,5},{10,8},{12,10},{14,12},{11,9},... | collective-permute-start | bytes 521000 | tf_op jit(solution)/shard_map/ppermute | solution.py:25
  36.6 8.4 %collective-permute-start.4 = (f32[6,18,3,134]{3,1,2,0:T(8,128)}, f32[6,18,3,134]{3,1,2,0:T(8,128)}, u32[]{:S(2)}, u32[]{:S(2)}) collective-permute-start(f32[6,18,3,134]{3,1,2,0:T(8,128)} %reverse_select_fusion.2), channel_id=1, source_target_pairs={{0,1},{1,0},{2,3},{3,2},{4,5},{5,4},{6,7},{7,6},{8,9},{9,8},{10,11... | collective-permute-start | bytes 521000 | tf_op jit(solution)/shard_map/ppermute | solution.py:32
  46.6 2.3 copy-start.14
  47.5 2.2 copy-start.1
  82.6 16.1 %copy-start.20 = (f32[12]{0:T(128)S(1)}, f32[12]{0:T(128)}, u32[]{:S(2)}) copy-start(f32[12]{0:T(128)} %get-tuple-element.416) | copy-start | bytes 148
  82.6 16.1 %copy-start.23 = (f32[16]{0:T(128)S(1)}, f32[16]{0:T(128)}, u32[]{:S(2)}) copy-start(f32[16]{0:T(128)} %get-tuple-element.411) | copy-start | bytes 196
  82.6 16.1 %copy-start.26 = (f32[16]{0:T(128)S(1)}, f32[16]{0:T(128)}, u32[]{:S(2)}) copy-start(f32[16]{0:T(128)} %get-tuple-element.412) | copy-start | bytes 196
  82.6 16.1 %copy-start.29 = (f32[16]{0:T(128)S(1)}, f32[16]{0:T(128)}, u32[]{:S(2)}) copy-start(f32[16]{0:T(128)} %get-tuple-element.415) | copy-start | bytes 196
  102.3 5.2 %collective-permute-start.7 = (f32[6,12,16,3]{2,1,3,0:T(8,128)S(1)}, f32[6,12,16,3]{2,1,3,0:T(8,128)S(1)}, u32[]{:S(2)}, u32[]{:S(2)}) collective-permute-start(f32[6,12,16,3]{2,1,3,0:T(8,128)S(1)} %copy.223), channel_id=1, source_target_pairs={{0,1},{1,0},{2,3},{3,2},{4,5},{5,4},{6,7},{7,6},{8,9},{9,8},{10,11... | collective-permute-start | bytes 41480 | tf_op jit(solution)/shard_map/ppermute | solution.py:22
  104.2 4.8 %collective-permute-start.8 = (f32[6,12,16,3]{2,1,3,0:T(8,128)S(1)}, f32[6,12,16,3]{2,1,3,0:T(8,128)S(1)}, u32[]{:S(2)}, u32[]{:S(2)}) collective-permute-start(f32[6,12,16,3]{2,1,3,0:T(8,128)S(1)} %copy.224), channel_id=1, source_target_pairs={{1,0},{0,1},{3,2},{2,3},{5,4},{4,5},{7,6},{6,7},{9,8},{8,9},{11,10... | collective-permute-start | bytes 41480 | tf_op jit(solution)/shard_map/ppermute | solution.py:25
  110.1 8.0 %collective-permute-start.10 = (f32[6,3,16,134]{3,2,1,0:T(8,128)S(1)}, f32[6,3,16,134]{3,2,1,0:T(8,128)S(1)}, u32[]{:S(2)}, u32[]{:S(2)}) collective-permute-start(f32[6,3,16,134]{3,2,1,0:T(8,128)S(1)} %get-tuple-element.386), channel_id=1, source_target_pairs={{8,0},{16,8},{24,16},{9,1},{17,9},{25,17},{10,2},{18,10},{26,18},{... | collective-permute-start | bytes 463112 | tf_op jit(solution)/shard_map/ppermute | solution.py:25
  112.0 7.3 %collective-permute-start.9 = (f32[6,3,16,134]{3,2,1,0:T(8,128)S(1)}, f32[6,3,16,134]{3,2,1,0:T(8,128)S(1)}, u32[]{:S(2)}, u32[]{:S(2)}) collective-permute-start(f32[6,3,16,134]{3,2,1,0:T(8,128)S(1)} %get-tuple-element.385), channel_id=1, source_target_pairs={{0,8},{8,16},{16,24},{1,9},{9,17},{17,25},{2,10},{10,18},{18,26},{... | collective-permute-start | bytes 463112 | tf_op jit(solution)/shard_map/ppermute | solution.py:22
  118.2 10.8 %copy-start.5 = (f32[6,3,16,134]{3,2,1,0:T(8,128)}, f32[6,3,16,134]{3,2,1,0:T(8,128)S(1)}, u32[]{:S(2)}) copy-start(f32[6,3,16,134]{3,2,1,0:T(8,128)S(1)} %collective-permute-done.10) | copy-start | bytes 463108
  119.3 9.6 %copy-start.9 = (f32[6,3,16,134]{3,2,1,0:T(8,128)}, f32[6,3,16,134]{3,2,1,0:T(8,128)S(1)}, u32[]{:S(2)}) copy-start(f32[6,3,16,134]{3,2,1,0:T(8,128)S(1)} %collective-permute-done.9) | copy-start | bytes 463108
  121.6 18.3 %collective-permute-start.12 = (f32[6,18,3,134]{3,1,2,0:T(8,128)}, f32[6,18,3,134]{3,1,2,0:T(8,128)}, u32[]{:S(2)}, u32[]{:S(2)}) collective-permute-start(f32[6,18,3,134]{3,1,2,0:T(8,128)} %copy.244), channel_id=1, source_target_pairs={{0,2},{2,4},{4,6},{1,3},{3,5},{5,7},{8,10},{10,12},{12,14},{9,11},... | collective-permute-start | bytes 521000 | tf_op jit(solution)/shard_map/ppermute | solution.py:22
  129.0 11.2 %collective-permute-start.13 = (f32[6,18,3,134]{3,1,2,0:T(8,128)}, f32[6,18,3,134]{3,1,2,0:T(8,128)}, u32[]{:S(2)}, u32[]{:S(2)}) collective-permute-start(f32[6,18,3,134]{3,1,2,0:T(8,128)} %copy.243), channel_id=1, source_target_pairs={{2,0},{4,2},{6,4},{3,1},{5,3},{7,5},{10,8},{12,10},{14,12},{11,9},... | collective-permute-start | bytes 521000 | tf_op jit(solution)/shard_map/ppermute | solution.py:25
  130.5 9.3 %collective-permute-start.11 = (f32[6,18,3,134]{3,1,2,0:T(8,128)}, f32[6,18,3,134]{3,1,2,0:T(8,128)}, u32[]{:S(2)}, u32[]{:S(2)}) collective-permute-start(f32[6,18,3,134]{3,1,2,0:T(8,128)} %reverse_select_fusion.1), channel_id=1, source_target_pairs={{0,1},{1,0},{2,3},{3,2},{4,5},{5,4},{6,7},{7,6},{8,9},{9,8},{10,11... | collective-permute-start | bytes 521000 | tf_op jit(solution)/shard_map/ppermute | solution.py:32
  134.2 7.6 %copy-start.6 = (f32[6,3,16,134]{3,2,1,0:T(8,128)S(1)}, f32[6,3,16,134]{3,2,1,0:T(8,128)}, u32[]{:S(2)}) copy-start(f32[6,3,16,134]{3,2,1,0:T(8,128)} %copy-done.5) | copy-start | bytes 463108
  134.2 7.6 %copy-start.10 = (f32[6,3,16,134]{3,2,1,0:T(8,128)S(1)}, f32[6,3,16,134]{3,2,1,0:T(8,128)}, u32[]{:S(2)}) copy-start(f32[6,3,16,134]{3,2,1,0:T(8,128)} %copy-done.9) | copy-start | bytes 463108
  141.8 2.3 copy-start.16
  142.7 2.2 copy-start.2
  187.8 16.1 %copy-start.21 = (f32[12]{0:T(128)S(1)}, f32[12]{0:T(128)}, u32[]{:S(2)}) copy-start(f32[12]{0:T(128)} %get-tuple-element.416) | copy-start | bytes 148
  187.8 16.1 %copy-start.24 = (f32[16]{0:T(128)S(1)}, f32[16]{0:T(128)}, u32[]{:S(2)}) copy-start(f32[16]{0:T(128)} %get-tuple-element.411) | copy-start | bytes 196
  187.8 16.1 %copy-start.27 = (f32[16]{0:T(128)S(1)}, f32[16]{0:T(128)}, u32[]{:S(2)}) copy-start(f32[16]{0:T(128)} %get-tuple-element.412) | copy-start | bytes 196
  187.8 16.1 %copy-start.30 = (f32[16]{0:T(128)S(1)}, f32[16]{0:T(128)}, u32[]{:S(2)}) copy-start(f32[16]{0:T(128)} %get-tuple-element.415) | copy-start | bytes 196
  208.4 5.5 %collective-permute-start.14 = (f32[6,12,16,3]{2,1,3,0:T(8,128)S(1)}, f32[6,12,16,3]{2,1,3,0:T(8,128)S(1)}, u32[]{:S(2)}, u32[]{:S(2)}) collective-permute-start(f32[6,12,16,3]{2,1,3,0:T(8,128)S(1)} %copy.231), channel_id=1, source_target_pairs={{0,1},{1,0},{2,3},{3,2},{4,5},{5,4},{6,7},{7,6},{8,9},{9,8},{10,11... | collective-permute-start | bytes 41480 | tf_op jit(solution)/shard_map/ppermute | solution.py:22
  209.7 5.7 %collective-permute-start.15 = (f32[6,12,16,3]{2,1,3,0:T(8,128)S(1)}, f32[6,12,16,3]{2,1,3,0:T(8,128)S(1)}, u32[]{:S(2)}, u32[]{:S(2)}) collective-permute-start(f32[6,12,16,3]{2,1,3,0:T(8,128)S(1)} %copy.232), channel_id=1, source_target_pairs={{1,0},{0,1},{3,2},{2,3},{5,4},{4,5},{7,6},{6,7},{9,8},{8,9},{11,10... | collective-permute-start | bytes 41480 | tf_op jit(solution)/shard_map/ppermute | solution.py:25
  216.5 7.5 %collective-permute-start.16 = (f32[6,3,16,134]{3,2,1,0:T(8,128)S(1)}, f32[6,3,16,134]{3,2,1,0:T(8,128)S(1)}, u32[]{:S(2)}, u32[]{:S(2)}) collective-permute-start(f32[6,3,16,134]{3,2,1,0:T(8,128)S(1)} %get-tuple-element.383), channel_id=1, source_target_pairs={{0,8},{8,16},{16,24},{1,9},{9,17},{17,25},{2,10},{10,18},{18,26},{... | collective-permute-start | bytes 463112 | tf_op jit(solution)/shard_map/ppermute | solution.py:22
  220.3 8.0 %collective-permute-start.17 = (f32[6,3,16,134]{3,2,1,0:T(8,128)S(1)}, f32[6,3,16,134]{3,2,1,0:T(8,128)S(1)}, u32[]{:S(2)}, u32[]{:S(2)}) collective-permute-start(f32[6,3,16,134]{3,2,1,0:T(8,128)S(1)} %get-tuple-element.384), channel_id=1, source_target_pairs={{8,0},{16,8},{24,16},{9,1},{17,9},{25,17},{10,2},{18,10},{26,18},{... | collective-permute-start | bytes 463112 | tf_op jit(solution)/shard_map/ppermute | solution.py:25
  223.9 13.4 %copy-start.3 = (f32[6,3,16,134]{3,2,1,0:T(8,128)}, f32[6,3,16,134]{3,2,1,0:T(8,128)S(1)}, u32[]{:S(2)}) copy-start(f32[6,3,16,134]{3,2,1,0:T(8,128)S(1)} %collective-permute-done.16) | copy-start | bytes 463108
  228.3 9.0 %copy-start.7 = (f32[6,3,16,134]{3,2,1,0:T(8,128)}, f32[6,3,16,134]{3,2,1,0:T(8,128)S(1)}, u32[]{:S(2)}) copy-start(f32[6,3,16,134]{3,2,1,0:T(8,128)S(1)} %collective-permute-done.17) | copy-start | bytes 463108
  230.5 16.8 %collective-permute-start.19 = (f32[6,18,3,134]{3,1,2,0:T(8,128)}, f32[6,18,3,134]{3,1,2,0:T(8,128)}, u32[]{:S(2)}, u32[]{:S(2)}) collective-permute-start(f32[6,18,3,134]{3,1,2,0:T(8,128)} %copy.246), channel_id=1, source_target_pairs={{0,2},{2,4},{4,6},{1,3},{3,5},{5,7},{8,10},{10,12},{12,14},{9,11},... | collective-permute-start | bytes 521000 | tf_op jit(solution)/shard_map/ppermute | solution.py:22
  237.4 10.3 %collective-permute-start.20 = (f32[6,18,3,134]{3,1,2,0:T(8,128)}, f32[6,18,3,134]{3,1,2,0:T(8,128)}, u32[]{:S(2)}, u32[]{:S(2)}) collective-permute-start(f32[6,18,3,134]{3,1,2,0:T(8,128)} %copy.245), channel_id=1, source_target_pairs={{2,0},{4,2},{6,4},{3,1},{5,3},{7,5},{10,8},{12,10},{14,12},{11,9},... | collective-permute-start | bytes 521000 | tf_op jit(solution)/shard_map/ppermute | solution.py:25
  238.9 8.5 %collective-permute-start.18 = (f32[6,18,3,134]{3,1,2,0:T(8,128)}, f32[6,18,3,134]{3,1,2,0:T(8,128)}, u32[]{:S(2)}, u32[]{:S(2)}) collective-permute-start(f32[6,18,3,134]{3,1,2,0:T(8,128)} %reverse_select_fusion), channel_id=1, source_target_pairs={{0,1},{1,0},{2,3},{3,2},{4,5},{5,4},{6,7},{7,6},{8,9},{9,8},{10,11... | collective-permute-start | bytes 521000 | tf_op jit(solution)/shard_map/ppermute | solution.py:32
  242.9 6.4 %copy-start.4 = (f32[6,3,16,134]{3,2,1,0:T(8,128)S(1)}, f32[6,3,16,134]{3,2,1,0:T(8,128)}, u32[]{:S(2)}) copy-start(f32[6,3,16,134]{3,2,1,0:T(8,128)} %copy-done.3) | copy-start | bytes 463108
  242.9 6.4 %copy-start.8 = (f32[6,3,16,134]{3,2,1,0:T(8,128)S(1)}, f32[6,3,16,134]{3,2,1,0:T(8,128)}, u32[]{:S(2)}) copy-start(f32[6,3,16,134]{3,2,1,0:T(8,128)} %copy-done.7) | copy-start | bytes 463108
  249.3 2.3 copy-start.15
  250.2 2.2 copy-start
  254.1 1.8 copy-start.19
  295.3 16.1 %copy-start.22 = (f32[12]{0:T(128)S(1)}, f32[12]{0:T(128)}, u32[]{:S(2)}) copy-start(f32[12]{0:T(128)} %get-tuple-element.416) | copy-start | bytes 148
  295.3 16.1 %copy-start.25 = (f32[16]{0:T(128)S(1)}, f32[16]{0:T(128)}, u32[]{:S(2)}) copy-start(f32[16]{0:T(128)} %get-tuple-element.411) | copy-start | bytes 196
  295.3 16.1 %copy-start.28 = (f32[16]{0:T(128)S(1)}, f32[16]{0:T(128)}, u32[]{:S(2)}) copy-start(f32[16]{0:T(128)} %get-tuple-element.412) | copy-start | bytes 196
  295.3 16.1 %copy-start.31 = (f32[16]{0:T(128)S(1)}, f32[16]{0:T(128)}, u32[]{:S(2)}) copy-start(f32[16]{0:T(128)} %get-tuple-element.415) | copy-start | bytes 196
  (8 other events, 9.9 us)
where the time goes:
time: 318 us; the launch traced here: 316 us
  other arithmetic  162 us (51%)
  local copies, waits for them, and re-layouts  64.2 us (20%)
  starting transfers between devices  44.6 us (14%)
  waiting for transfers between devices  43.4 us (14%)
    dynamic_update_slice x54, other arithmetic, face_fluxes(): lax.map(lambda couple: interface(couple[0], couple[1], axis), (fluxes, fi...  67.4 us
    mul x54, other arithmetic, interface(): plus_part = 0.5 * (flux + wave_speed * field)  53.5 us
    ppermute x9, starting transfers between devices, padded_2(): lax.ppermute(lax.slice_in_dim(block, block.shape[dim] - width, None, axis...  30.2 us
    unnamed x94, local copies, waits for them, and re-layouts  20.4 us
    ppermute x9, waiting for transfers between devices, padded_2(): lax.ppermute(lax.slice_in_dim(block, 0, width, axis=dim), axis, backward)  16.5 us
    ppermute x3, waiting for transfers between devices, from_behind(): lax.ppermute(array, axis, [(i, (i + by) % length) for i in range(length)])  16 us
    ppermute x9, starting transfers between devices, padded_2(): lax.ppermute(lax.slice_in_dim(block, 0, width, axis=dim), axis, backward)  11.6 us
    ppermute x9, waiting for transfers between devices, padded_2(): lax.ppermute(lax.slice_in_dim(block, block.shape[dim] - width, None, axis...  11 us
  transfers between devices with their start and end apart: 21, of which 17 were waited for; matrix products, arithmetic and copies ran while one was open for 6% of the time, Pallas kernels for 0%

commit v1 on v0

v1 whole, which is shorter than its diff:
```python
import functools
import math

import jax
import jax.numpy as jnp
from jax import lax
from jax.experimental import pallas as pl
from jax.experimental.pallas import tpu as pltpu
from jax.sharding import PartitionSpec as P

hole_mass = 1.0
inner_radius = 1.8
wave_speed = 1.25
courant = 0.3
smooth_eps = 1e-06

G = 3
HALF = 0.5 * wave_speed
EPS = smooth_eps / (HALF * HALF)

B1, B3, D1, D3, B2, D2 = range(6)
E3, NE1, NH3, H1, E2, NH2 = range(6)
FROM_ARGS = ((0, 0), (0, 2), (1, 0), (1, 2), (0, 1), (1, 1))
RADIAL = {B1: None, B3: (E2, 1), D1: None, D3: (NH2, 1), B2: (E3, -1), D2: (NH3, -1)}
PHI_U = (B1, B2, D1, D2, B3, D3)
PHI_E = (E2, NE1, NH2, H1)
PARITY = {B1: 1.0, B3: -1.0, D1: 1.0, D3: -1.0, B2: -1.0, D2: -1.0}


class Lazy:
    def __init__(self, make):
        self.make, self.kept = make, {}

    def __call__(self, k):
        if k not in self.kept:
            self.kept[k] = self.make(k)
        return self.kept[k]


class Rough:
    def __init__(self, value):
        self.diff = Lazy(lambda k: value(k + 1) - value(k))
        self.second = Lazy(lambda k: self.diff(k) - self.diff(k - 1))
        self.third = Lazy(lambda k: self.second(k + 1) - self.second(k))
        self.twice = Lazy(lambda k: self.second(k) + self.second(k))
        self.mid = Lazy(
            lambda k: (self.twice(k) * self.twice(k)) * (1.0 / 3.0)
            + (self.diff(k) * self.diff(k - 1) + EPS)
        )
        self.sq_low = Lazy(lambda k: square(self.mid(k) + self.diff(k) * self.twice(k)))
        self.sq_mid = Lazy(lambda k: square(self.mid(k)))
        self.sq_high = Lazy(lambda k: square(self.mid(k) - self.diff(k - 1) * self.twice(k)))


def square(x):
    return x * x


def correction(outer, mid, inner, third_outer, third_mid):
    outer3 = 3.0 * outer
    inner2 = inner + inner
    top = mid * (inner2 * third_outer + outer3 * third_mid)
    bottom = mid * (inner + outer3) + outer3 * inner2
    return top / bottom


def walk(faces, get_u, get_e, sign, emit):
    u = Lazy(get_u)
    if get_e is None:
        plus = minus = Rough(u)
    else:
        e = Lazy(get_e)
        total = Lazy(lambda k: e(k) + u(k))
        gap = Lazy(lambda k: e(k) - u(k))
        plus, minus = (Rough(total), Rough(gap)) if sign > 0 else (Rough(gap), Rough(total))
    previous = None
    for f in range(faces):
        i = f + 2
        left = correction(
            plus.sq_low(i - 1), plus.sq_mid(i), plus.sq_high(i + 1),
            plus.third(i - 1), plus.third(i),
        )
        right = correction(
            minus.sq_high(i + 2), minus.sq_mid(i + 1), minus.sq_low(i),
            minus.third(i + 1), minus.third(i),
        )
        if get_e is None:
            flux = (plus.third(i) - left) - right
        else:
            flux = (
                (7.0 * (e(i) + e(i + 1)) - (e(i - 1) + e(i + 2)))
                + 0.5 * (plus.third(i) - minus.third(i))
            ) + (right - left)
        if f:
            emit(f - 1, previous, flux)
        previous = flux


def fields_of(c, a, s):
    return (
        a * c[D3] + s * c[B2],
        -(a * c[D1]),
        s * c[D2] - a * c[B3],
        a * c[B1],
        a * c[D2] - s * c[B3],
        -(a * c[B2] + s * c[D3]),
    )


class Sizes:
    def __init__(self, rows, thetas, phis):
        self.R, self.T, self.L = rows, thetas, phis
        self.slices = 6 * rows
        self.per = self.L // self.T
        self.n_u = self.slices // self.per
        self.n_e = 4 * rows // self.per
        self.n_t = self.n_u + self.n_e
        self.step = self.L // 8
        self.k_a = 0
        self.k_s = rows + 2 * G
        self.k_rp = 2 * self.k_s
        self.k_rm = self.k_rp + rows
        self.k_tp = self.k_rm + rows
        self.k_tm = self.k_tp + thetas
        self.k_par = -(-(self.k_tm + thetas) // 8) * 8
        self.k_n = self.k_par + self.slices

    def check(self):
        assert self.T % 8 == 0 and self.L % self.T == 0 and self.L == 128
        assert (4 * self.R) % 8 == 0 and (2 * self.R) % 8 == 0
        assert (4 * self.R) % self.per == 0 and (2 * self.R) % self.per == 0


def prep(z, scal, co, u_ref, e_ref, pt_ref, ra_ref, rb_ref, ta_ref, tb_ref, p_ref):
    R, T, L = z.R, z.T, z.L

    def fields_at(r, carry):
        a = co[pl.ds(z.k_a + G + r, 1), :]
        s = co[pl.ds(z.k_s + G + r, 1), :]
        for t in range(0, T, 8):
            row = pl.multiple_of(r * T + t, 8)
            c = [u_ref[pl.ds(k * R * T + row, 8), :] for k in range(6)]
            for k, value in enumerate(fields_of(c, a, s)):
                e_ref[pl.ds(k * R * T + row, 8), :] = value
        return carry

    lax.fori_loop(0, R, fields_at, 0, unroll=2)

    def turned(ref, comps, block):
        parts = []
        for n in range(block * z.per, (block + 1) * z.per):
            row = (comps[n // R] * R + n % R) * T
            parts.append(ref[row : row + T, :])
        return jnp.concatenate(parts, axis=0).T

    for b in range(z.n_u):
        pt_ref[b] = turned(u_ref, PHI_U, b)
    for b in range(z.n_e):
        pt_ref[z.n_u + b] = turned(e_ref, PHI_E, b)
    flat = pt_ref.reshape(z.n_t * L, L)
    for k in range(G):
        for n in range(0, z.n_t, 8):
            m = min(8, z.n_t - n)
            p_ref[k, n : n + m, :] = flat[pl.ds(n * L + k, m, stride=L), :]
            p_ref[G + k, n : n + m, :] = flat[pl.ds(n * L + L - G + k, m, stride=L), :]

    def rows_to(ref, start):
        for c in range(6):
            ref[c * G * T : (c + 1) * G * T, :] = u_ref[
                (c * R + start) * T : (c * R + start + G) * T, :
            ]

    def polar_to(ref, picks, flip):
        for k, pick in enumerate(picks):
            for n in range(0, z.slices, 8):
                value = u_ref[pl.ds(n * T + pick, 8, stride=T), :]
                if flip:
                    value = value * co[z.k_par + n : z.k_par + n + 8, :]
                ref[k * z.slices + n : k * z.slices + n + 8, :] = value

    row_even, theta_even, north, south = scal[0] == 1, scal[1] == 1, scal[2] == 1, scal[3] == 1

    def low_polar(ref):
        pl.when(north)(lambda: polar_to(ref, (2, 1, 0), True))
        pl.when(jnp.logical_not(north))(lambda: polar_to(ref, (0, 1, 2), False))

    def high_polar(ref):
        pl.when(south)(lambda: polar_to(ref, (T - 1, T - 2, T - 3), True))
        pl.when(jnp.logical_not(south))(lambda: polar_to(ref, (T - 3, T - 2, T - 1), False))

    @pl.when(row_even)
    def _():
        rows_to(ra_ref, R - G)
        rows_to(rb_ref, 0)

    @pl.when(jnp.logical_not(row_even))
    def _():
        rows_to(ra_ref, 0)
        rows_to(rb_ref, R - G)

    @pl.when(theta_even)
    def _():
        low_polar(ta_ref)
        high_polar(tb_ref)

    @pl.when(jnp.logical_not(theta_even))
    def _():
        low_polar(tb_ref)
        high_polar(ta_ref)


def first_kernel(z, scal, co, m_ref, d_ref, *outs):
    u_ref = outs[0]
    n = z.R * z.T
    for c, (which, k) in enumerate(FROM_ARGS):
        u_ref[c * n : (c + 1) * n, :] = (m_ref, d_ref)[which][k * n : (k + 1) * n, :]
    prep(z, scal, co, *outs)


def stage_kernel(z, weight, last, step_phi, *refs):
    refs = list(refs)
    scal, co, u_ref, e_ref, pt_ref, ra, rb, ta, tb, pr = refs[:10]
    refs = refs[10:]
    u0_ref = None
    if weight:
        u0_ref = refs.pop(0)
    if last:
        m_ref, d_ref = refs[:2]
        refs = refs[2:]
    else:
        outs = refs[:8]
        refs = refs[8:]
    new, pad, turned, acc_p, acc_t, rows_u, rows_e, pol_u, pol_e = refs
    R, T, L = z.R, z.T, z.L
    row_even, theta_even = scal[0] == 1, scal[1] == 1

    def pad_block(b, carry):
        pad[b, 8 : 8 + L, :] = pt_ref[b]
        return carry

    lax.fori_loop(0, z.n_t, pad_block, 0)
    tall = L + 16
    flat = pad.reshape(z.n_t * tall, L)
    for k in range(G):
        for n in range(0, z.n_t, 8):
            m = min(8, z.n_t - n)
            flat[pl.ds(n * tall + 8 + L + k, m, stride=tall), :] = pr[k, n : n + m, :]
            flat[pl.ds(n * tall + 8 - G + k, m, stride=tall), :] = pr[G + k, n : n + m, :]

    def phi_block(b, carry, has_e):
        def at(block):
            return lambda k: pad[block, pl.ds(8 - G + k, 8, stride=z.step), :]

        scale = -step_phi if has_e else step_phi

        def emit(j, low, high):
            turned[pl.ds(j, 8, stride=z.step), :] = scale * (high - low)

        walk(z.step + 1, at(b), at(z.n_u + b) if has_e else None, -1, emit)
        acc_p[pl.ds(pl.multiple_of(b * L, L), L), :] = turned[...].T
        return carry

    lax.fori_loop(0, z.n_e, functools.partial(phi_block, has_e=True), 0)
    lax.fori_loop(z.n_e, z.n_u, functools.partial(phi_block, has_e=False), 0)

    def polar_in(low, high):
        pol_u[0 : G * z.slices, :] = low[...]
        pol_u[G * z.slices :, :] = high[...]

    pl.when(theta_even)(lambda: polar_in(ta, tb))
    pl.when(jnp.logical_not(theta_even))(lambda: polar_in(tb, ta))
    for k in range(2 * G):
        c = [pol_u[k * z.slices + n * R : k * z.slices + (n + 1) * R, :] for n in range(6)]
        a = co[z.k_a + G : z.k_a + G + R, :]
        s = co[z.k_s + G : z.k_s + G + R, :]
        for n, value in enumerate(fields_of(c, a, s)[:4]):
            pol_e[(k * 4 + n) * R : (k * 4 + n + 1) * R, :] = value

    def theta_group(g, carry, has_e):
        def at(ref, ghosts, per):
            def get(k):
                if G <= k < G + T:
                    return ref[pl.ds(g * 8 * T + (k - G), 8, stride=T), :]
                ghost = k if k < G else k - T
                return ghosts[pl.ds(pl.multiple_of(ghost * per + g * 8, 8), 8), :]

            return get

        def emit(j, low, high):
            acc_t[pl.ds(g * 8 * T + j, 8, stride=T), :] = (
                co[z.k_tp + j : z.k_tp + j + 1, :] * high
                - co[z.k_tm + j : z.k_tm + j + 1, :] * low
            )

        get_e = at(e_ref, pol_e, 4 * R) if has_e else None
        walk(T + 1, at(u_ref, pol_u, z.slices), get_e, 1, emit)
        return carry

    lax.fori_loop(0, 4 * R // 8, functools.partial(theta_group, has_e=True), 0)
    lax.fori_loop(4 * R // 8, z.slices // 8, functools.partial(theta_group, has_e=False), 0)

    def rows_in(low, high):
        for c in range(6):
            span = slice(c * G * T, (c + 1) * G * T)
            rows_u[2 * c * G * T : (2 * c + 1) * G * T, :] = low[span, :]
            rows_u[(2 * c + 1) * G * T : (2 * c + 2) * G * T, :] = high[span, :]

    pl.when(row_even)(lambda: rows_in(rb, ra))
    pl.when(jnp.logical_not(row_even))(lambda: rows_in(ra, rb))
    for k in range(2 * G):
        r = k if k < G else k + R
        a = co[z.k_a + r : z.k_a + r + 1, :]
        s = co[z.k_s + r : z.k_s + r + 1, :]
        for t in range(0, T, 8):
            c = [rows_u[(2 * G * n + k) * T + t : (2 * G * n + k) * T + t + 8, :] for n in range(6)]
            values = fields_of(c, a, s)
            for n in (E3, NH3, E2, NH2):
                rows_e[(2 * G * n + k) * T + t : (2 * G * n + k) * T + t + 8, :] = values[n]

    def radial_tile(t, carry):
        base = pl.multiple_of(t * 8, 8)
        for c in range(6):
            def at(ref, ghosts, n):
                def get(k):
                    if G <= k < G + R:
                        return ref[pl.ds((n * R + k - G) * T + base, 8), :]
                    ghost = k if k < G else k - R
                    return ghosts[pl.ds((2 * G * n + ghost) * T + base, 8), :]

                return get

            spec = RADIAL[c]
            sign = spec[1] if spec else 1

            def emit(j, low, high):
                row = (c * R + j) * T + base
                across = (PHI_U.index(c) * R + j) * T + base
                inc = (
                    co[z.k_rp + j : z.k_rp + j + 1, :] * high
                    - co[z.k_rm + j : z.k_rm + j + 1, :] * low
                )
                rest = acc_t[pl.ds(row, 8), :] + acc_p[pl.ds(across, 8), :]
                inc = rest + inc if sign > 0 else rest - inc
                value = u_ref[pl.ds(row, 8), :] + inc
                if weight:
                    value = (1.0 - weight) * value + weight * u0_ref[pl.ds(row, 8), :]
                new[pl.ds(row, 8), :] = value

            get_e = at(e_ref, rows_e, spec[0]) if spec else None
            walk(R + 1, at(u_ref, rows_u, c), get_e, sign, emit)
        return carry

    lax.fori_loop(0, T // 8, radial_tile, 0)

    n = R * T

    def project(i, carry):
        row = pl.multiple_of(i * 8, 8)
        c = [new[pl.ds(k * n + row, 8), :] for k in range(6)]
        b = (c[B1], c[B2], c[B3])
        d = (c[D1], c[D2], c[D3])
        b_square = jnp.maximum(b[0] * b[0] + b[1] * b[1] + b[2] * b[2], 1.0)
        along = (b[0] * d[0] + b[1] * d[1] + b[2] * d[2]) / b_square
        d = [dk - along * bk for dk, bk in zip(d, b)]
        d_square = d[0] * d[0] + d[1] * d[1] + d[2] * d[2]
        shrink = jnp.sqrt(b_square / jnp.maximum(d_square, b_square))
        d = [dk * shrink for dk in d]
        if last:
            for k in range(3):
                m_ref[pl.ds(k * n + row, 8), :] = b[k]
                d_ref[pl.ds(k * n + row, 8), :] = d[k]
        else:
            for k, value in zip((B1, B2, B3, D1, D2, D3), (*b, *d)):
                outs[0][pl.ds(k * n + row, 8), :] = value
        return carry

    lax.fori_loop(0, n // 8, project, 0, unroll=4)
    if not last:
        prep(z, scal, co, *outs)


def body(mesh, magnetic, electric):
    n_row, n_theta, n_phi = (mesh.shape[k] for k in ("row", "theta", "phi"))
    _, R, T, L = magnetic.shape
    z = Sizes(R, T, L)
    z.check()
    f32 = jnp.float32
    d_theta = math.pi / (T * n_theta)
    d_phi = 2.0 * math.pi / (L * n_phi)
    step_dt = courant / (2.0 / d_theta + 1.0 / d_phi)
    unit = -step_dt * HALF / 6.0

    i_row, i_theta = lax.axis_index("row"), lax.axis_index("theta")
    scal = jnp.stack(
        [(i_row % 2 == 0), (i_theta % 2 == 0), (i_theta == 0), (i_theta == n_theta - 1)]
    ).astype(jnp.int32)
    radii = inner_radius + ((i_row * R - G + jnp.arange(R + 2 * G)).astype(f32) + 0.5) * d_theta
    angles = ((i_theta * T - G + jnp.arange(T + 2 * G)).astype(f32) + 0.5) * d_theta
    ratio = 2.0 * hole_mass / radii
    lapse = 1.0 / jnp.sqrt(1.0 + ratio) / wave_speed
    shift = ratio / (1.0 + ratio) / wave_speed
    r_face = (0.5 * (radii[G - 1 : -G] + radii[G : 1 - G])) ** 2
    r_scale = unit / (radii[G:-G] ** 2 * d_theta)
    t_face = jnp.sin(0.5 * (angles[G - 1 : -G] + angles[G : 1 - G]))
    t_scale = unit / (jnp.sin(angles[G:-G]) * d_theta)
    parity = jnp.repeat(jnp.array([PARITY[c] for c in range(6)], f32), R)
    parts = [
        lapse, shift, r_face[1:] * r_scale, r_face[:-1] * r_scale,
        t_face[1:] * t_scale, t_face[:-1] * t_scale,
    ]
    used = sum(p.shape[0] for p in parts)
    table = jnp.concatenate(parts + [jnp.zeros((z.k_par - used,), f32), parity])
    co = jnp.broadcast_to(table[:, None], (z.k_n, L))

    vmem = pl.BlockSpec(memory_space=pltpu.VMEM)
    smem = pl.BlockSpec(memory_space=pltpu.SMEM)
    whole = (z.slices * T, L)
    state_shapes = [
        whole, whole, (z.n_t, L, L),
        (6 * G * T, L), (6 * G * T, L), (G * z.slices, L), (G * z.slices, L), (2 * G, z.n_t, L),
    ]
    state_out = [jax.ShapeDtypeStruct(s, f32) for s in state_shapes]
    half_out = [jax.ShapeDtypeStruct((3 * R * T, L), f32)] * 2
    scratch = [
        pltpu.VMEM(whole, f32),
        pltpu.VMEM((z.n_t, L + 16, L), f32),
        pltpu.VMEM((L, L), f32),
        pltpu.VMEM(whole, f32),
        pltpu.VMEM(whole, f32),
        pltpu.VMEM((6 * 2 * G * T, L), f32),
        pltpu.VMEM((6 * 2 * G * T, L), f32),
        pltpu.VMEM((2 * G * z.slices, L), f32),
        pltpu.VMEM((2 * G * 4 * R, L), f32),
    ]

    row_a = [p for k in range(0, n_row - 1, 2) for p in ((k, k + 1), (k + 1, k))]
    row_b = [p for k in range(1, n_row - 1, 2) for p in ((k, k + 1), (k + 1, k))]

    def polar_pairs(odd):
        pairs = []
        for k in range(-1, n_theta):
            if k % 2 != odd:
                continue
            for p in range(n_phi):
                if k in (-1, n_theta - 1):
                    t = max(k, 0)
                    pairs.append((t * n_phi + p, t * n_phi + (p + n_phi // 2) % n_phi))
                else:
                    low, high = k * n_phi + p, (k + 1) * n_phi + p
                    pairs += [(low, high), (high, low)]
        return pairs

    def exchange(ra, rb, ta, tb, p):
        left = [(k, (k - 1) % n_phi) for k in range(n_phi)]
        right = [(k, (k + 1) % n_phi) for k in range(n_phi)]
        if n_phi == 2:
            p = lax.ppermute(p, "phi", left)
        else:
            p = jnp.concatenate(
                [lax.ppermute(p[:G], "phi", left), lax.ppermute(p[G:], "phi", right)]
            )
        return (
            lax.ppermute(ra, "row", row_a),
            lax.ppermute(rb, "row", row_b),
            lax.ppermute(ta, ("theta", "phi"), polar_pairs(1)),
            lax.ppermute(tb, ("theta", "phi"), polar_pairs(0)),
            p,
        )

    state = pl.pallas_call(
        functools.partial(first_kernel, z),
        out_shape=state_out,
        in_specs=[smem, vmem, vmem, vmem],
        out_specs=[vmem] * 8,
        name="first",
    )(scal, co, magnetic.reshape(-1, L), electric.reshape(-1, L))
    start = state[0]
    weights = (0.0, 0.75, 1.0 / 3.0)
    for n, weight in enumerate(weights):
        last = n == len(weights) - 1
        extra = [start] if weight else []
        state = pl.pallas_call(
            functools.partial(stage_kernel, z, weight, last, unit / d_phi),
            out_shape=half_out if last else state_out,
            in_specs=[smem] + [vmem] * (9 + len(extra)),
            out_specs=[vmem] * (2 if last else 8),
            scratch_shapes=scratch,
            name=f"stage{n}",
        )(scal, co, *state[:3], *exchange(*state[3:]), *extra)
    return tuple(s.reshape(magnetic.shape) for s in state)


def solution(mesh):
    spec = P(None, "row", "theta", "phi")
    return jax.shard_map(
        functools.partial(body, mesh),
        mesh=mesh, in_specs=(spec, spec), out_specs=(spec, spec), check_vma=False,
    )
```

time: 318 us -> 66.2 us (0.21)
  other arithmetic: 162 us -> 1.22 us
  local copies, waits for them, and re-layouts: 64.2 us -> 3.77 us
  waiting for transfers between devices: 43.4 us -> 7.41 us
  Pallas kernels: 0 us -> 31.7 us
  starting transfers between devices: 44.6 us -> 21 us
    dynamic_update_slice x54 -> x0, other arithmetic: 67.4 us -> none  [face_fluxes(): lax.map(lambda couple: interface(couple[0], couple[1], axis), (fluxes, fi...]
    mul x55 -> x5, other arithmetic: 53.5 us -> 0.35 us  [the longest x1 0.12 us: body(): t_face[:-1] * t_scale]
    ppermute x21 -> x15, waiting for transfers between devices: 43.4 us -> 7.41 us  [the longest x3 7.38 us: exchange(): p = lax.ppermute(p, 'phi', left)]
    pallas_call x0 -> x4, Pallas kernels: none -> 31.7 us  [the longest x3 28.5 us: body(): pl.pallas_call(functools.partial(stage_kernel, z, weight, last, unit / d_...]
    slice x23 -> x0, local copies, waits for them, and re-layouts: 29 us -> none  [the longest x3 8.21 us: tendency(): polar_flux[:, 3:-3, :, 3:-3]]
    ppermute x21 -> x15, starting transfers between devices: 44.6 us -> 21 us  [the longest x3 12.3 us: exchange(): lax.ppermute(rb, 'row', row_b)]
    unnamed x94 -> x32, local copies, waits for them, and re-layouts: 20.4 us -> 2.82 us
    select_n x9 -> x0, other arithmetic: 10.1 us -> none  [the longest x3 5.88 us: body(): outgoing = jnp.where(theta_index == 0, north_rows, south_rows)]
  transfers between devices with their start and end apart: 21 -> 15, of which waited for: 17 -> 3; matrix products, arithmetic and copies ran while one was open for 6% -> 0% of each run, Pallas kernels for 0% -> 0%
where the time goes in v1:
time: 66.2 us; the launch traced here: 65.9 us
  Pallas kernels  31.7 us (48%)
  starting transfers between devices  21 us (32%)
  waiting for transfers between devices  7.41 us (11%)
  local copies, waits for them, and re-layouts  3.77 us (6%)
  other arithmetic  1.22 us (2%)
  between operations  0.9 us (1%)
    pallas_call x3, Pallas kernels, body(): pl.pallas_call(functools.partial(stage_kernel, z, weight, last, unit / d_...  28.5 us
    ppermute x3, starting transfers between devices, exchange(): lax.ppermute(rb, 'row', row_b)  12.3 us
    ppermute x3, waiting for transfers between devices, exchange(): p = lax.ppermute(p, 'phi', left)  7.38 us
    pallas_call x1, Pallas kernels, body(): pl.pallas_call(functools.partial(first_kernel, z), out_shape=state_out, i...  3.2 us
    ppermute x3, starting transfers between devices, exchange(): lax.ppermute(tb, ('theta', 'phi'), polar_pairs(0))  3.04 us
    ppermute x3, starting transfers between devices, exchange(): lax.ppermute(ta, ('theta', 'phi'), polar_pairs(1))  2.9 us
    unnamed x32, local copies, waits for them, and re-layouts  2.82 us
    ppermute x3, starting transfers between devices, exchange(): p = lax.ppermute(p, 'phi', left)  2.63 us
  transfers between devices with their start and end apart: 15, of which 3 were waited for; matrix products, arithmetic and copies ran while one was open for 0% of the time, Pallas kernels for 0%

profile of v1, /device:TPU:1, one launch (start us, length us, event | category | flops | bytes accessed | tf_op | source)
XLA Modules:
  0.0 65.9 jit_solution(7090160872050125747)
XLA Ops:
  0.7 0.1 multiply_sine_fusion
  0.8 0.1 multiply_multiply_fusion
  0.9 0.1 slice_multiply_fusion.2
  1.0 0.1 slice_multiply_fusion.3
  1.1 0.1 slice_multiply_fusion
  1.2 0.1 slice_multiply_fusion.1
  1.3 0.6 copy-done.15
  1.9 0.1 broadcast_in_dim.4
  1.9 0.1 reshape.20
  2.0 0.7 add_convert_fusion.scal.refs_0_
  2.7 0.1 concatenate.3
  2.7 0.7 %broadcast_in_dim.10.co.refs_1_ = f32[168,128]{1,0:T(8,128)} broadcast(f32[168]{0:T(256)S(1)} %concatenate.3), dimensions={0} | broadcast | bytes 86688 | tf_op jit(solution)/shard_map/broadcast_in_dim | solution.py:413
  3.5 3.2 %first.1 = (f32[1152,128]{1,0:T(8,128)}, f32[1152,128]{1,0:T(8,128)}, f32[15,128,128]{2,1,0:T(8,128)}, f32[288,128]{1,0:T(8,128)}, f32[288,128]{1,0:T(8,128)}, /...) custom-call(s32[4]{0:T(128)} %add_convert_fusion.scal.refs_0_, ...), custom_call_target="tpu_custom_call" | custom-call | tf_op jit(solution)/shard_map/first/pallas_call | solution.py:470
  6.7 4.5 %collective-permute-start.1 = (f32[288,128]{1,0:T(8,128)}, f32[288,128]{1,0:T(8,128)S(1)}, u32[]{:S(2)}, u32[]{:S(2)}) collective-permute-start(f32[288,128]{1,0:T(8,128)} %get-tuple-element.32), channel_id=1, source_target_pairs={{8,16},{16,8},{9,17},{17,9},{10,18},{18,10},{11,19},{19,11},{12,20... | collective-permute-start | bytes 442376 | tf_op jit(solution)/shard_map/ppermute | solution.py:464
  11.1 1.3 %collective-permute-start.2 = (f32[216,128]{1,0:T(8,128)}, f32[216,128]{1,0:T(8,128)S(1)}, u32[]{:S(2)}, u32[]{:S(2)}) collective-permute-start(f32[216,128]{1,0:T(8,128)} %get-tuple-element.33), channel_id=1, source_target_pairs={{0,1},{1,0},{2,4},{4,2},{3,5},{5,3},{6,7},{7,6},{8,9},{9,8},{10,12... | collective-permute-start | bytes 331784 | tf_op jit(solution)/shard_map/ppermute | solution.py:465
  12.4 1.3 %collective-permute-start.3 = (f32[216,128]{1,0:T(8,128)}, f32[216,128]{1,0:T(8,128)S(1)}, u32[]{:S(2)}, u32[]{:S(2)}) collective-permute-start(f32[216,128]{1,0:T(8,128)} %get-tuple-element.34), channel_id=1, source_target_pairs={{0,2},{2,0},{1,3},{3,1},{4,6},{6,4},{5,7},{7,5},{8,10},{10,8},{9,1... | collective-permute-start | bytes 331784 | tf_op jit(solution)/shard_map/ppermute | solution.py:466
  13.8 1.2 %collective-permute-start.4 = (f32[6,15,128]{2,1,0:T(8,128)}, f32[6,15,128]{2,1,0:T(8,128)S(1)}, u32[]{:S(2)}, u32[]{:S(2)}) collective-permute-start(f32[6,15,128]{2,1,0:T(8,128)} %get-tuple-element.35), channel_id=1, source_target_pairs={{0,1},{1,0},{2,3},{3,2},{4,5},{5,4},{6,7},{7,6},{8,9},{9,8},{10,11... | collective-permute-start | bytes 138248 | tf_op jit(solution)/shard_map/ppermute | solution.py:457
  15.0 1.9 %collective-permute-done.4.refs_9_ = f32[6,15,128]{2,1,0:T(8,128)S(1)} collective-permute-done((f32[6,15,128]{2,1,0:T(8,128)}, f32[6,15,128]{2,1,0:T(8,128)S(1)}, u32[]{:S(2)}, u32[]{:S(2)}) %collective-permute-start.4) | collective-permute-done | bytes 46112 | tf_op jit(solution)/shard_map/ppermute | solution.py:457
  17.0 0.6 copy-done.13
  17.6 0.0 copy-done.7
  17.6 0.1 copy-done.10
  17.7 0.0 copy-done.1
  17.7 0.0 copy-done.4
  17.7 9.7 %stage0.1 = (f32[1152,128]{1,0:T(8,128)}, f32[1152,128]{1,0:T(8,128)}, f32[15,128,128]{2,1,0:T(8,128)}, f32[288,128]{1,0:T(8,128)}, f32[288,128]{1,0:T(8,128)}, ...) custom-call(s32[4]{0:T(128)} %add_convert_fusion.scal.refs_0_, ...), custom_call_target="tpu_custom_call" | custom-call | tf_op jit(solution)/shard_map/stage0/pallas_call | solution.py:482
  27.5 0.0 collective-permute-start.5
  27.5 4.2 %collective-permute-start.6 = (f32[288,128]{1,0:T(8,128)}, f32[288,128]{1,0:T(8,128)S(1)}, u32[]{:S(2)}, u32[]{:S(2)}) collective-permute-start(f32[288,128]{1,0:T(8,128)} %get-tuple-element.40), channel_id=1, source_target_pairs={{8,16},{16,8},{9,17},{17,9},{10,18},{18,10},{11,19},{19,11},{12,20... | collective-permute-start | bytes 442376 | tf_op jit(solution)/shard_map/ppermute | solution.py:464
  31.7 1.3 %collective-permute-start.7 = (f32[216,128]{1,0:T(8,128)}, f32[216,128]{1,0:T(8,128)S(1)}, u32[]{:S(2)}, u32[]{:S(2)}) collective-permute-start(f32[216,128]{1,0:T(8,128)} %get-tuple-element.41), channel_id=1, source_target_pairs={{0,1},{1,0},{2,4},{4,2},{3,5},{5,3},{6,7},{7,6},{8,9},{9,8},{10,12... | collective-permute-start | bytes 331784 | tf_op jit(solution)/shard_map/ppermute | solution.py:465
  33.0 1.3 %collective-permute-start.8 = (f32[216,128]{1,0:T(8,128)}, f32[216,128]{1,0:T(8,128)S(1)}, u32[]{:S(2)}, u32[]{:S(2)}) collective-permute-start(f32[216,128]{1,0:T(8,128)} %get-tuple-element.42), channel_id=1, source_target_pairs={{0,2},{2,0},{1,3},{3,1},{4,6},{6,4},{5,7},{7,5},{8,10},{10,8},{9,1... | collective-permute-start | bytes 331784 | tf_op jit(solution)/shard_map/ppermute | solution.py:466
  34.3 0.2 collective-permute-start.9
  34.6 2.9 %collective-permute-done.9.refs_9_ = f32[6,15,128]{2,1,0:T(8,128)S(1)} collective-permute-done((f32[6,15,128]{2,1,0:T(8,128)}, f32[6,15,128]{2,1,0:T(8,128)S(1)}, u32[]{:S(2)}, u32[]{:S(2)}) %collective-permute-start.9) | collective-permute-done | bytes 46112 | tf_op jit(solution)/shard_map/ppermute | solution.py:457
  37.6 0.6 copy-done.12
  38.1 0.1 copy-done.6
  38.2 0.1 copy-done.8
  38.2 0.0 copy-done
  38.2 0.0 copy-done.2
  38.3 10.0 %stage1.1 = (f32[1152,128]{1,0:T(8,128)}, f32[1152,128]{1,0:T(8,128)}, f32[15,128,128]{2,1,0:T(8,128)}, f32[288,128]{1,0:T(8,128)}, f32[288,128]{1,0:T(8,128)}, ...) custom-call(s32[4]{0:T(128)} %add_convert_fusion.scal.refs_0_, ...), custom_call_target="tpu_custom_call" | custom-call | tf_op jit(solution)/shard_map/stage1/pallas_call | solution.py:482
  48.3 0.0 collective-permute-start.10
  48.4 3.6 %collective-permute-start.11 = (f32[288,128]{1,0:T(8,128)}, f32[288,128]{1,0:T(8,128)S(1)}, u32[]{:S(2)}, u32[]{:S(2)}) collective-permute-start(f32[288,128]{1,0:T(8,128)} %get-tuple-element.48), channel_id=1, source_target_pairs={{8,16},{16,8},{9,17},{17,9},{10,18},{18,10},{11,19},{19,11},{12,20... | collective-permute-start | bytes 442376 | tf_op jit(solution)/shard_map/ppermute | solution.py:464
  52.0 0.3 collective-permute-start.12
  52.3 0.4 collective-permute-start.13
  52.7 1.2 %collective-permute-start.14 = (f32[6,15,128]{2,1,0:T(8,128)}, f32[6,15,128]{2,1,0:T(8,128)S(1)}, u32[]{:S(2)}, u32[]{:S(2)}) collective-permute-start(f32[6,15,128]{2,1,0:T(8,128)} %get-tuple-element.51), channel_id=1, source_target_pairs={{0,1},{1,0},{2,3},{3,2},{4,5},{5,4},{6,7},{7,6},{8,9},{9,8},{10,11... | collective-permute-start | bytes 138248 | tf_op jit(solution)/shard_map/ppermute | solution.py:457
  53.9 2.5 %collective-permute-done.14.refs_9_ = f32[6,15,128]{2,1,0:T(8,128)S(1)} collective-permute-done((f32[6,15,128]{2,1,0:T(8,128)}, f32[6,15,128]{2,1,0:T(8,128)S(1)}, u32[]{:S(2)}, u32[]{:S(2)}) %collective-permute-start.14) | collective-permute-done | bytes 46112 | tf_op jit(solution)/shard_map/ppermute | solution.py:457
  56.5 0.5 copy-done.14
  57.0 0.1 copy-done.9
  57.1 0.0 copy-done.11
  57.1 0.0 copy-done.3
  57.1 0.1 copy-done.5
  57.2 8.7 %stage2.1 = (f32[576,128]{1,0:T(8,128)}, f32[576,128]{1,0:T(8,128)}) custom-call(s32[4]{0:T(128)} %add_convert_fusion.scal.refs_0_, f32[168,128]{1,0:T(8,128)} %broadcast_in_dim.10.co.refs_1_, f32[1152,128]{1,0:T(8,128)} %get-tuple-element.44.refs_2_, f32[1152,128]{1,0:T(8,128)} %get-tuple-element.45.refs_3_, f32[15,128,128]{2,1,0:T(8,128)} %get-tuple-element.46.refs_4_, ...), custom_call_target="tpu_custom_call" | custom-call | tf_op jit(solution)/shard_map/stage2/pallas_call | solution.py:482
  (33 shorter events, 0.1 us)
Async XLA Ops:
  1.2 0.7 %copy-start.15 = (f32[6]{0:T(128)S(1)}, f32[6]{0:T(128)}, u32[]{:S(2)}) copy-start(f32[6]{0:T(128)} %constant.63.clone) | copy-start | bytes 76
  6.7 10.3 %collective-permute-start = (f32[288,128]{1,0:T(8,128)}, f32[288,128]{1,0:T(8,128)S(1)}, u32[]{:S(2)}, u32[]{:S(2)}) collective-permute-start(f32[288,128]{1,0:T(8,128)} %get-tuple-element.31), channel_id=1, source_target_pairs={{0,8},{8,0},{16,24},{24,16},{1,9},{9,1},{17,25},{25,17},{2,10},{10... | collective-permute-start | bytes 442376 | tf_op jit(solution)/shard_map/ppermute | solution.py:463
  6.7 10.3 %collective-permute-start.1 = (f32[288,128]{1,0:T(8,128)}, f32[288,128]{1,0:T(8,128)S(1)}, u32[]{:S(2)}, u32[]{:S(2)}) collective-permute-start(f32[288,128]{1,0:T(8,128)} %get-tuple-element.32), channel_id=1, source_target_pairs={{8,16},{16,8},{9,17},{17,9},{10,18},{18,10},{11,19},{19,11},{12,20... | collective-permute-start | bytes 442376 | tf_op jit(solution)/shard_map/ppermute | solution.py:464
  11.1 5.8 %collective-permute-start.2 = (f32[216,128]{1,0:T(8,128)}, f32[216,128]{1,0:T(8,128)S(1)}, u32[]{:S(2)}, u32[]{:S(2)}) collective-permute-start(f32[216,128]{1,0:T(8,128)} %get-tuple-element.33), channel_id=1, source_target_pairs={{0,1},{1,0},{2,4},{4,2},{3,5},{5,3},{6,7},{7,6},{8,9},{9,8},{10,12... | collective-permute-start | bytes 331784 | tf_op jit(solution)/shard_map/ppermute | solution.py:465
  12.4 4.5 %collective-permute-start.3 = (f32[216,128]{1,0:T(8,128)}, f32[216,128]{1,0:T(8,128)S(1)}, u32[]{:S(2)}, u32[]{:S(2)}) collective-permute-start(f32[216,128]{1,0:T(8,128)} %get-tuple-element.34), channel_id=1, source_target_pairs={{0,2},{2,0},{1,3},{3,1},{4,6},{6,4},{5,7},{7,5},{8,10},{10,8},{9,1... | collective-permute-start | bytes 331784 | tf_op jit(solution)/shard_map/ppermute | solution.py:466
  13.8 3.2 %collective-permute-start.4 = (f32[6,15,128]{2,1,0:T(8,128)}, f32[6,15,128]{2,1,0:T(8,128)S(1)}, u32[]{:S(2)}, u32[]{:S(2)}) collective-permute-start(f32[6,15,128]{2,1,0:T(8,128)} %get-tuple-element.35), channel_id=1, source_target_pairs={{0,1},{1,0},{2,3},{3,2},{4,5},{5,4},{6,7},{7,6},{8,9},{9,8},{10,11... | collective-permute-start | bytes 138248 | tf_op jit(solution)/shard_map/ppermute | solution.py:457
  16.9 0.6 copy-start.13
  17.0 0.6 copy-start.7
  17.0 0.7 %copy-start.10 = (f32[216,128]{1,0:T(8,128)}, f32[216,128]{1,0:T(8,128)S(1)}, u32[]{:S(2)}) copy-start(f32[216,128]{1,0:T(8,128)S(1)} %collective-permute-done.3.refs_8_) | copy-start | bytes 331780
  17.0 0.7 %copy-start.1 = (f32[288,128]{1,0:T(8,128)}, f32[288,128]{1,0:T(8,128)S(1)}, u32[]{:S(2)}) copy-start(f32[288,128]{1,0:T(8,128)S(1)} %collective-permute-done.refs_5_) | copy-start | bytes 442372
  17.0 0.7 %copy-start.4 = (f32[288,128]{1,0:T(8,128)}, f32[288,128]{1,0:T(8,128)S(1)}, u32[]{:S(2)}) copy-start(f32[288,128]{1,0:T(8,128)S(1)} %collective-permute-done.1.refs_6_) | copy-start | bytes 442372
  27.5 10.1 %collective-permute-start.5 = (f32[288,128]{1,0:T(8,128)}, f32[288,128]{1,0:T(8,128)S(1)}, u32[]{:S(2)}, u32[]{:S(2)}) collective-permute-start(f32[288,128]{1,0:T(8,128)} %get-tuple-element.39), channel_id=1, source_target_pairs={{0,8},{8,0},{16,24},{24,16},{1,9},{9,1},{17,25},{25,17},{2,10},{10... | collective-permute-start | bytes 442376 | tf_op jit(solution)/shard_map/ppermute | solution.py:463
  27.5 10.0 %collective-permute-start.6 = (f32[288,128]{1,0:T(8,128)}, f32[288,128]{1,0:T(8,128)S(1)}, u32[]{:S(2)}, u32[]{:S(2)}) collective-permute-start(f32[288,128]{1,0:T(8,128)} %get-tuple-element.40), channel_id=1, source_target_pairs={{8,16},{16,8},{9,17},{17,9},{10,18},{18,10},{11,19},{19,11},{12,20... | collective-permute-start | bytes 442376 | tf_op jit(solution)/shard_map/ppermute | solution.py:464
  31.7 5.8 %collective-permute-start.7 = (f32[216,128]{1,0:T(8,128)}, f32[216,128]{1,0:T(8,128)S(1)}, u32[]{:S(2)}, u32[]{:S(2)}) collective-permute-start(f32[216,128]{1,0:T(8,128)} %get-tuple-element.41), channel_id=1, source_target_pairs={{0,1},{1,0},{2,4},{4,2},{3,5},{5,3},{6,7},{7,6},{8,9},{9,8},{10,12... | collective-permute-start | bytes 331784 | tf_op jit(solution)/shard_map/ppermute | solution.py:465
  33.0 4.5 %collective-permute-start.8 = (f32[216,128]{1,0:T(8,128)}, f32[216,128]{1,0:T(8,128)S(1)}, u32[]{:S(2)}, u32[]{:S(2)}) collective-permute-start(f32[216,128]{1,0:T(8,128)} %get-tuple-element.42), channel_id=1, source_target_pairs={{0,2},{2,0},{1,3},{3,1},{4,6},{6,4},{5,7},{7,5},{8,10},{10,8},{9,1... | collective-permute-start | bytes 331784 | tf_op jit(solution)/shard_map/ppermute | solution.py:466
  34.3 3.2 %collective-permute-start.9 = (f32[6,15,128]{2,1,0:T(8,128)}, f32[6,15,128]{2,1,0:T(8,128)S(1)}, u32[]{:S(2)}, u32[]{:S(2)}) collective-permute-start(f32[6,15,128]{2,1,0:T(8,128)} %get-tuple-element.43), channel_id=1, source_target_pairs={{0,1},{1,0},{2,3},{3,2},{4,5},{5,4},{6,7},{7,6},{8,9},{9,8},{10,11... | collective-permute-start | bytes 138248 | tf_op jit(solution)/shard_map/ppermute | solution.py:457
  37.5 0.6 copy-start.12
  37.5 0.7 %copy-start.6 = (f32[216,128]{1,0:T(8,128)}, f32[216,128]{1,0:T(8,128)S(1)}, u32[]{:S(2)}) copy-start(f32[216,128]{1,0:T(8,128)S(1)} %collective-permute-done.7.refs_7_) | copy-start | bytes 331780
  37.5 0.7 %copy-start.8 = (f32[216,128]{1,0:T(8,128)}, f32[216,128]{1,0:T(8,128)S(1)}, u32[]{:S(2)}) copy-start(f32[216,128]{1,0:T(8,128)S(1)} %collective-permute-done.8.refs_8_) | copy-start | bytes 331780
  37.5 0.7 %copy-start = (f32[288,128]{1,0:T(8,128)}, f32[288,128]{1,0:T(8,128)S(1)}, u32[]{:S(2)}) copy-start(f32[288,128]{1,0:T(8,128)S(1)} %collective-permute-done.5.refs_5_) | copy-start | bytes 442372
  37.6 0.7 %copy-start.2 = (f32[288,128]{1,0:T(8,128)}, f32[288,128]{1,0:T(8,128)S(1)}, u32[]{:S(2)}) copy-start(f32[288,128]{1,0:T(8,128)S(1)} %collective-permute-done.6.refs_6_) | copy-start | bytes 442372
  48.3 8.1 %collective-permute-start.10 = (f32[288,128]{1,0:T(8,128)}, f32[288,128]{1,0:T(8,128)S(1)}, u32[]{:S(2)}, u32[]{:S(2)}) collective-permute-start(f32[288,128]{1,0:T(8,128)} %get-tuple-element.47), channel_id=1, source_target_pairs={{0,8},{8,0},{16,24},{24,16},{1,9},{9,1},{17,25},{25,17},{2,10},{10... | collective-permute-start | bytes 442376 | tf_op jit(solution)/shard_map/ppermute | solution.py:463
  48.4 8.1 %collective-permute-start.11 = (f32[288,128]{1,0:T(8,128)}, f32[288,128]{1,0:T(8,128)S(1)}, u32[]{:S(2)}, u32[]{:S(2)}) collective-permute-start(f32[288,128]{1,0:T(8,128)} %get-tuple-element.48), channel_id=1, source_target_pairs={{8,16},{16,8},{9,17},{17,9},{10,18},{18,10},{11,19},{19,11},{12,20... | collective-permute-start | bytes 442376 | tf_op jit(solution)/shard_map/ppermute | solution.py:464
  52.0 4.4 %collective-permute-start.12 = (f32[216,128]{1,0:T(8,128)}, f32[216,128]{1,0:T(8,128)S(1)}, u32[]{:S(2)}, u32[]{:S(2)}) collective-permute-start(f32[216,128]{1,0:T(8,128)} %get-tuple-element.49), channel_id=1, source_target_pairs={{0,1},{1,0},{2,4},{4,2},{3,5},{5,3},{6,7},{7,6},{8,9},{9,8},{10,12... | collective-permute-start | bytes 331784 | tf_op jit(solution)/shard_map/ppermute | solution.py:465
  52.3 4.1 %collective-permute-start.13 = (f32[216,128]{1,0:T(8,128)}, f32[216,128]{1,0:T(8,128)S(1)}, u32[]{:S(2)}, u32[]{:S(2)}) collective-permute-start(f32[216,128]{1,0:T(8,128)} %get-tuple-element.50), channel_id=1, source_target_pairs={{0,2},{2,0},{1,3},{3,1},{4,6},{6,4},{5,7},{7,5},{8,10},{10,8},{9,1... | collective-permute-start | bytes 331784 | tf_op jit(solution)/shard_map/ppermute | solution.py:466
  52.7 3.7 %collective-permute-start.14 = (f32[6,15,128]{2,1,0:T(8,128)}, f32[6,15,128]{2,1,0:T(8,128)S(1)}, u32[]{:S(2)}, u32[]{:S(2)}) collective-permute-start(f32[6,15,128]{2,1,0:T(8,128)} %get-tuple-element.51), channel_id=1, source_target_pairs={{0,1},{1,0},{2,3},{3,2},{4,5},{5,4},{6,7},{7,6},{8,9},{9,8},{10,11... | collective-permute-start | bytes 138248 | tf_op jit(solution)/shard_map/ppermute | solution.py:457
  56.4 0.6 copy-start.14
  56.4 0.7 %copy-start.9 = (f32[216,128]{1,0:T(8,128)}, f32[216,128]{1,0:T(8,128)S(1)}, u32[]{:S(2)}) copy-start(f32[216,128]{1,0:T(8,128)S(1)} %collective-permute-done.12.refs_7_) | copy-start | bytes 331780
  56.4 0.7 %copy-start.11 = (f32[216,128]{1,0:T(8,128)}, f32[216,128]{1,0:T(8,128)S(1)}, u32[]{:S(2)}) copy-start(f32[216,128]{1,0:T(8,128)S(1)} %collective-permute-done.13.refs_8_) | copy-start | bytes 331780
  56.4 0.7 %copy-start.3 = (f32[288,128]{1,0:T(8,128)}, f32[288,128]{1,0:T(8,128)S(1)}, u32[]{:S(2)}) copy-start(f32[288,128]{1,0:T(8,128)S(1)} %collective-permute-done.10.refs_5_) | copy-start | bytes 442372
  56.5 0.8 %copy-start.5 = (f32[288,128]{1,0:T(8,128)}, f32[288,128]{1,0:T(8,128)S(1)}, u32[]{:S(2)}) copy-start(f32[288,128]{1,0:T(8,128)S(1)} %collective-permute-done.11.refs_6_) | copy-start | bytes 442372

commit v2 on v1

--- a/solution.py
+++ b/solution.py
@@ -15,6 +15,7 @@
 smooth_eps = 1e-06
 
 G = 3
+VMEM_LIMIT = 24 * 2**20
 HALF = 0.5 * wave_speed
 EPS = smooth_eps / (HALF * HALF)
 
@@ -108,7 +109,8 @@
 
 
 class Sizes:
-    def __init__(self, rows, thetas, phis):
+    def __init__(self, mesh, rows, thetas, phis):
+        self.n_row, self.n_theta, self.n_phi = (mesh.shape[k] for k in ("row", "theta", "phi"))
         self.R, self.T, self.L = rows, thetas, phis
         self.slices = 6 * rows
         self.per = self.L // self.T
@@ -116,22 +118,68 @@
         self.n_e = 4 * rows // self.per
         self.n_t = self.n_u + self.n_e
         self.step = self.L // 8
-        self.k_a = 0
-        self.k_s = rows + 2 * G
-        self.k_rp = 2 * self.k_s
-        self.k_rm = self.k_rp + rows
-        self.k_tp = self.k_rm + rows
-        self.k_tm = self.k_tp + thetas
-        self.k_par = -(-(self.k_tm + thetas) // 8) * 8
-        self.k_n = self.k_par + self.slices
+        self.d_theta = math.pi / (thetas * self.n_theta)
+        self.d_phi = 2.0 * math.pi / (phis * self.n_phi)
+        step_dt = courant / (2.0 / self.d_theta + 1.0 / self.d_phi)
+        self.unit = -step_dt * HALF / 6.0
+        at = 0
+        for name, count in (
+            ("k_a", rows + 2 * G), ("k_s", rows + 2 * G), ("k_rp", rows), ("k_rm", rows),
+            ("k_tp", thetas), ("k_tm", thetas), ("k_par", self.slices),
+        ):
+            setattr(self, name, at)
+            at += -(-count // 8) * 8
+        self.k_n = at
 
     def check(self):
         assert self.T % 8 == 0 and self.L % self.T == 0 and self.L == 128
+        assert self.T == self.step
         assert (4 * self.R) % 8 == 0 and (2 * self.R) % 8 == 0
         assert (4 * self.R) % self.per == 0 and (2 * self.R) % self.per == 0
 
 
-def prep(z, scal, co, u_ref, e_ref, pt_ref, ra_ref, rb_ref, ta_ref, tb_ref, p_ref):
+def table(z, co):
+    R, T, L = z.R, z.T, z.L
+    f32 = jnp.float32
+
+    def rows(count):
+        return lax.broadcasted_iota(jnp.int32, (-(-count // 8) * 8, L), 0)
+
+    def radius(count, first):
+        row = rows(count) + (lax.axis_index("row") * R + first)
+        return inner_radius + (row.astype(f32) + 0.5) * z.d_theta
+
+    def angle(count, first):
+        row = rows(count) + (lax.axis_index("theta") * T + first)
+        return (row.astype(f32) + 0.5) * z.d_theta
+
+    def put(at, value):
+        co[at : at + value.shape[0], :] = value
+
+    ratio = 2.0 * hole_mass / radius(R + 2 * G, -G)
+    put(z.k_a, 1.0 / jnp.sqrt(1.0 + ratio) / wave_speed)
+    put(z.k_s, ratio / (1.0 + ratio) / wave_speed)
+    low, mid, high = (radius(R, k) for k in (-1, 0, 1))
+    scale = z.unit / (mid * mid * z.d_theta)
+    put(z.k_rp, square(0.5 * (mid + high)) * scale)
+    put(z.k_rm, square(0.5 * (low + mid)) * scale)
+    low, mid, high = (angle(T, k) for k in (-1, 0, 1))
+    scale = z.unit / (jnp.sin(mid) * z.d_theta)
+    put(z.k_tp, jnp.sin(0.5 * (mid + high)) * scale)
+    put(z.k_tm, jnp.sin(0.5 * (low + mid)) * scale)
+    for c in range(6):
+        co[z.k_par + c * R : z.k_par + (c + 1) * R, :] = jnp.full((R, L), PARITY[c], f32)
+
+
+RADIAL_E = (E3, NH3, E2, NH2)
+
+
+def conditions(z):
+    row, theta = lax.axis_index("row"), lax.axis_index("theta")
+    return row % 2 == 0, theta % 2 == 0, theta == 0, theta == z.n_theta - 1
+
+
+def prep(z, co, u_ref, e_ref, ut_ref, et_ref, pt_ref, ra_ref, rb_ref, ta_ref, tb_ref, p_ref, nat):
     R, T, L = z.R, z.T, z.L
 
     def fields_at(r, carry):
@@ -140,29 +188,37 @@
         for t in range(0, T, 8):
             row = pl.multiple_of(r * T + t, 8)
             c = [u_ref[pl.ds(k * R * T + row, 8), :] for k in range(6)]
-            for k, value in enumerate(fields_of(c, a, s)):
-                e_ref[pl.ds(k * R * T + row, 8), :] = value
+            values = fields_of(c, a, s)
+            for n, k in enumerate(RADIAL_E):
+                e_ref[pl.ds(n * R * T + row, 8), :] = values[k]
+            for n, k in enumerate(PHI_E):
+                nat[pl.ds(n * R * T + row, 8), :] = values[k]
+            for k in range(6):
+                ut_ref[pl.ds(t * z.slices + k * R + r, 8, stride=z.slices), :] = c[k]
+            for k in range(4):
+                et_ref[pl.ds(t * 4 * R + k * R + r, 8, stride=4 * R), :] = values[k]
         return carry
 
     lax.fori_loop(0, R, fields_at, 0, unroll=2)
 
-    def turned(ref, comps, block):
+    def turn(ref, comps, block, into):
         parts = []
         for n in range(block * z.per, (block + 1) * z.per):
             row = (comps[n // R] * R + n % R) * T
             parts.append(ref[row : row + T, :])
-        return jnp.concatenate(parts, axis=0).T
+        value = jnp.concatenate(parts, axis=0).T
+        for n in range(0, L, 8):
+            pt_ref[into, pl.ds((n % z.step) * 8 + n // z.step, 8, stride=8), :] = value[n : n + 8]
 
     for b in range(z.n_u):
-        pt_ref[b] = turned(u_ref, PHI_U, b)
+        turn(u_ref, PHI_U, b, b)
     for b in range(z.n_e):
-        pt_ref[z.n_u + b] = turned(e_ref, PHI_E, b)
-    flat = pt_ref.reshape(z.n_t * L, L)
-    for k in range(G):
-        for n in range(0, z.n_t, 8):
-            m = min(8, z.n_t - n)
-            p_ref[k, n : n + m, :] = flat[pl.ds(n * L + k, m, stride=L), :]
-            p_ref[G + k, n : n + m, :] = flat[pl.ds(n * L + L - G + k, m, stride=L), :]
+        turn(nat, range(4), b, z.n_u + b)
+    for b in range(z.n_t):
+        for k in range(G):
+            p_ref[k, b : b + 1, :] = pt_ref[b, 8 * k : 8 * k + 1, :]
+            row = 8 * (z.step - G + k) + 7
+            p_ref[G + k, b : b + 1, :] = pt_ref[b, row : row + 1, :]
 
     def rows_to(ref, start):
         for c in range(6):
@@ -171,14 +227,12 @@
             ]
 
     def polar_to(ref, picks, flip):
+        parity = co[z.k_par : z.k_par + z.slices, :] if flip else None
         for k, pick in enumerate(picks):
-            for n in range(0, z.slices, 8):
-                value = u_ref[pl.ds(n * T + pick, 8, stride=T), :]
-                if flip:
-                    value = value * co[z.k_par + n : z.k_par + n + 8, :]
-                ref[k * z.slices + n : k * z.slices + n + 8, :] = value
-
-    row_even, theta_even, north, south = scal[0] == 1, scal[1] == 1, scal[2] == 1, scal[3] == 1
+            value = ut_ref[pick * z.slices : (pick + 1) * z.slices, :]
+            ref[k * z.slices : (k + 1) * z.slices, :] = value * parity if flip else value
+
+    row_even, theta_even, north, south = conditions(z)
 
     def low_polar(ref):
         pl.when(north)(lambda: polar_to(ref, (2, 1, 0), True))
@@ -209,18 +263,19 @@
         high_polar(ta_ref)
 
 
-def first_kernel(z, scal, co, m_ref, d_ref, *outs):
-    u_ref = outs[0]
+def first_kernel(z, m_ref, d_ref, co, *rest):
+    table(z, co)
+    u_ref = rest[0]
     n = z.R * z.T
     for c, (which, k) in enumerate(FROM_ARGS):
         u_ref[c * n : (c + 1) * n, :] = (m_ref, d_ref)[which][k * n : (k + 1) * n, :]
-    prep(z, scal, co, *outs)
-
-
-def stage_kernel(z, weight, last, step_phi, *refs):
+    prep(z, co, *rest)
+
+
+def stage_kernel(z, weight, last, *refs):
     refs = list(refs)
-    scal, co, u_ref, e_ref, pt_ref, ra, rb, ta, tb, pr = refs[:10]
-    refs = refs[10:]
+    co, u_ref, e_ref, ut, et, pt, ra, rb, ta, tb, pr = refs[:11]
+    refs = refs[11:]
     u0_ref = None
     if weight:
         u0_ref = refs.pop(0)
@@ -228,40 +283,46 @@
         m_ref, d_ref = refs[:2]
         refs = refs[2:]
     else:
-        outs = refs[:8]
-        refs = refs[8:]
-    new, pad, turned, acc_p, acc_t, rows_u, rows_e, pol_u, pol_e = refs
+        outs = refs[:10]
+        refs = refs[10:]
+    new, turned, acc_p, acc_t, rows_u, rows_e, pol_u, pol_e = refs
     R, T, L = z.R, z.T, z.L
-    row_even, theta_even = scal[0] == 1, scal[1] == 1
-
-    def pad_block(b, carry):
-        pad[b, 8 : 8 + L, :] = pt_ref[b]
-        return carry
-
-    lax.fori_loop(0, z.n_t, pad_block, 0)
-    tall = L + 16
-    flat = pad.reshape(z.n_t * tall, L)
-    for k in range(G):
-        for n in range(0, z.n_t, 8):
-            m = min(8, z.n_t - n)
-            flat[pl.ds(n * tall + 8 + L + k, m, stride=tall), :] = pr[k, n : n + m, :]
-            flat[pl.ds(n * tall + 8 - G + k, m, stride=tall), :] = pr[G + k, n : n + m, :]
+    row_even, theta_even, _, _ = conditions(z)
+
+    lane_row = lax.broadcasted_iota(jnp.int32, (8, L), 0)
 
     def phi_block(b, carry, has_e):
         def at(block):
-            return lambda k: pad[block, pl.ds(8 - G + k, 8, stride=z.step), :]
-
-        scale = -step_phi if has_e else step_phi
+            def get(k):
+                cell = k - G
+                wrapped = cell % z.step
+                value = pt[block, 8 * wrapped : 8 * wrapped + 8, :]
+                if cell < 0:
+                    ghost = pr[G + k, pl.ds(block, 1), :]
+                    value = jnp.where(lane_row == 0, ghost, pltpu.roll(value, 1, 0))
+                elif cell >= z.step:
+                    ghost = pr[cell - z.step, pl.ds(block, 1), :]
+                    value = jnp.where(lane_row == 7, ghost, pltpu.roll(value, 7, 0))
+                return value
+
+            return get
+
+        scale = -z.unit / z.d_phi if has_e else z.unit / z.d_phi
 
         def emit(j, low, high):
-            turned[pl.ds(j, 8, stride=z.step), :] = scale * (high - low)
+            turned[b, 8 * j : 8 * j + 8, :] = scale * (high - low)
 
         walk(z.step + 1, at(b), at(z.n_u + b) if has_e else None, -1, emit)
-        acc_p[pl.ds(pl.multiple_of(b * L, L), L), :] = turned[...].T
         return carry
 
     lax.fori_loop(0, z.n_e, functools.partial(phi_block, has_e=True), 0)
     lax.fori_loop(z.n_e, z.n_u, functools.partial(phi_block, has_e=False), 0)
+    for b in range(z.n_u):
+        parts = [
+            turned[b, pl.ds((n % z.step) * 8 + n // z.step, 8, stride=8), :]
+            for n in range(0, L, 8)
+        ]
+        acc_p[b * L : (b + 1) * L, :] = jnp.concatenate(parts, axis=0).T
 
     def polar_in(low, high):
         pol_u[0 : G * z.slices, :] = low[...]
@@ -277,23 +338,25 @@
             pol_e[(k * 4 + n) * R : (k * 4 + n + 1) * R, :] = value
 
     def theta_group(g, carry, has_e):
+        base = pl.multiple_of(g * 8, 8)
+
         def at(ref, ghosts, per):
             def get(k):
                 if G <= k < G + T:
-                    return ref[pl.ds(g * 8 * T + (k - G), 8, stride=T), :]
+                    return ref[pl.ds((k - G) * per + base, 8), :]
                 ghost = k if k < G else k - T
-                return ghosts[pl.ds(pl.multiple_of(ghost * per + g * 8, 8), 8), :]
+                return ghosts[pl.ds(ghost * per + base, 8), :]
 
             return get
 
         def emit(j, low, high):
-            acc_t[pl.ds(g * 8 * T + j, 8, stride=T), :] = (
+            acc_t[pl.ds(j * z.slices + base, 8), :] = (
                 co[z.k_tp + j : z.k_tp + j + 1, :] * high
                 - co[z.k_tm + j : z.k_tm + j + 1, :] * low
             )
 
-        get_e = at(e_ref, pol_e, 4 * R) if has_e else None
-        walk(T + 1, at(u_ref, pol_u, z.slices), get_e, 1, emit)
+        get_e = at(et, pol_e, 4 * R) if has_e else None
+        walk(T + 1, at(ut, pol_u, z.slices), get_e, 1, emit)
         return carry
 
     lax.fori_loop(0, 4 * R // 8, functools.partial(theta_group, has_e=True), 0)
@@ -314,8 +377,8 @@
         for t in range(0, T, 8):
             c = [rows_u[(2 * G * n + k) * T + t : (2 * G * n + k) * T + t + 8, :] for n in range(6)]
             values = fields_of(c, a, s)
-            for n in (E3, NH3, E2, NH2):
-                rows_e[(2 * G * n + k) * T + t : (2 * G * n + k) * T + t + 8, :] = values[n]
+            for n, field in enumerate(RADIAL_E):
+                rows_e[(2 * G * n + k) * T + t : (2 * G * n + k) * T + t + 8, :] = values[field]
 
     def radial_tile(t, carry):
         base = pl.multiple_of(t * 8, 8)
@@ -339,14 +402,15 @@
                     co[z.k_rp + j : z.k_rp + j + 1, :] * high
                     - co[z.k_rm + j : z.k_rm + j + 1, :] * low
                 )
-                rest = acc_t[pl.ds(row, 8), :] + acc_p[pl.ds(across, 8), :]
+                polar = acc_t[pl.ds(base * z.slices + c * R + j, 8, stride=z.slices), :]
+                rest = polar + acc_p[pl.ds(across, 8), :]
                 inc = rest + inc if sign > 0 else rest - inc
                 value = u_ref[pl.ds(row, 8), :] + inc
                 if weight:
                     value = (1.0 - weight) * value + weight * u0_ref[pl.ds(row, 8), :]
                 new[pl.ds(row, 8), :] = value
 
-            get_e = at(e_ref, rows_e, spec[0]) if spec else None
+            get_e = at(e_ref, rows_e, RADIAL_E.index(spec[0])) if spec else None
             walk(R + 1, at(u_ref, rows_u, c), get_e, sign, emit)
         return carry
 
@@ -376,62 +440,35 @@
 
     lax.fori_loop(0, n // 8, project, 0, unroll=4)
     if not last:
-        prep(z, scal, co, *outs)
+        prep(z, co, *outs, acc_p)
 
 
 def body(mesh, magnetic, electric):
-    n_row, n_theta, n_phi = (mesh.shape[k] for k in ("row", "theta", "phi"))
     _, R, T, L = magnetic.shape
-    z = Sizes(R, T, L)
+    z = Sizes(mesh, R, T, L)
     z.check()
+    n_row, n_theta, n_phi = z.n_row, z.n_theta, z.n_phi
     f32 = jnp.float32
-    d_theta = math.pi / (T * n_theta)
-    d_phi = 2.0 * math.pi / (L * n_phi)
-    step_dt = courant / (2.0 / d_theta + 1.0 / d_phi)
-    unit = -step_dt * HALF / 6.0
-
-    i_row, i_theta = lax.axis_index("row"), lax.axis_index("theta")
-    scal = jnp.stack(
-        [(i_row % 2 == 0), (i_theta % 2 == 0), (i_theta == 0), (i_theta == n_theta - 1)]
-    ).astype(jnp.int32)
-    radii = inner_radius + ((i_row * R - G + jnp.arange(R + 2 * G)).astype(f32) + 0.5) * d_theta
-    angles = ((i_theta * T - G + jnp.arange(T + 2 * G)).astype(f32) + 0.5) * d_theta
-    ratio = 2.0 * hole_mass / radii
-    lapse = 1.0 / jnp.sqrt(1.0 + ratio) / wave_speed
-    shift = ratio / (1.0 + ratio) / wave_speed
-    r_face = (0.5 * (radii[G - 1 : -G] + radii[G : 1 - G])) ** 2
-    r_scale = unit / (radii[G:-G] ** 2 * d_theta)
-    t_face = jnp.sin(0.5 * (angles[G - 1 : -G] + angles[G : 1 - G]))
-    t_scale = unit / (jnp.sin(angles[G:-G]) * d_theta)
-    parity = jnp.repeat(jnp.array([PARITY[c] for c in range(6)], f32), R)
-    parts = [
-        lapse, shift, r_face[1:] * r_scale, r_face[:-1] * r_scale,
-        t_face[1:] * t_scale, t_face[:-1] * t_scale,
-    ]
-    used = sum(p.shape[0] for p in parts)
-    table = jnp.concatenate(parts + [jnp.zeros((z.k_par - used,), f32), parity])
-    co = jnp.broadcast_to(table[:, None], (z.k_n, L))
-
     vmem = pl.BlockSpec(memory_space=pltpu.VMEM)
-    smem = pl.BlockSpec(memory_space=pltpu.SMEM)
     whole = (z.slices * T, L)
+    part = (4 * R * T, L)
     state_shapes = [
-        whole, whole, (z.n_t, L, L),
+        whole, part, whole, part, (z.n_t, L, L),
         (6 * G * T, L), (6 * G * T, L), (G * z.slices, L), (G * z.slices, L), (2 * G, z.n_t, L),
     ]
     state_out = [jax.ShapeDtypeStruct(s, f32) for s in state_shapes]
     half_out = [jax.ShapeDtypeStruct((3 * R * T, L), f32)] * 2
     scratch = [
         pltpu.VMEM(whole, f32),
-        pltpu.VMEM((z.n_t, L + 16, L), f32),
-        pltpu.VMEM((L, L), f32),
+        pltpu.VMEM((z.n_u, L, L), f32),
         pltpu.VMEM(whole, f32),
         pltpu.VMEM(whole, f32),
         pltpu.VMEM((6 * 2 * G * T, L), f32),
-        pltpu.VMEM((6 * 2 * G * T, L), f32),
+        pltpu.VMEM((4 * 2 * G * T, L), f32),
         pltpu.VMEM((2 * G * z.slices, L), f32),
         pltpu.VMEM((2 * G * 4 * R, L), f32),
     ]
+    params = pltpu.CompilerParams(vmem_limit_bytes=VMEM_LIMIT)
 
     row_a = [p for k in range(0, n_row - 1, 2) for p in ((k, k + 1), (k + 1, k))]
     row_b = [p for k in range(1, n_row - 1, 2) for p in ((k, k + 1), (k + 1, k))]
@@ -467,26 +504,29 @@
             p,
         )
 
-    state = pl.pallas_call(
+    co, *state = pl.pallas_call(
         functools.partial(first_kernel, z),
-        out_shape=state_out,
-        in_specs=[smem, vmem, vmem, vmem],
-        out_specs=[vmem] * 8,
+        out_shape=[jax.ShapeDtypeStruct((z.k_n, L), f32)] + state_out,
+        in_specs=[vmem] * 2,
+        out_specs=[vmem] * 11,
+        scratch_shapes=[pltpu.VMEM(part, f32)],
+        compiler_params=params,
         name="first",
-    )(scal, co, magnetic.reshape(-1, L), electric.reshape(-1, L))
+    )(magnetic.reshape(-1, L), electric.reshape(-1, L))
     start = state[0]
     weights = (0.0, 0.75, 1.0 / 3.0)
     for n, weight in enumerate(weights):
         last = n == len(weights) - 1
         extra = [start] if weight else []
         state = pl.pallas_call(
-            functools.partial(stage_kernel, z, weight, last, unit / d_phi),
+            functools.partial(stage_kernel, z, weight, last),
             out_shape=half_out if last else state_out,
-            in_specs=[smem] + [vmem] * (9 + len(extra)),
-            out_specs=[vmem] * (2 if last else 8),
+            in_specs=[vmem] * (11 + len(extra)),
+            out_specs=[vmem] * (2 if last else 10),
             scratch_shapes=scratch,
+            compiler_params=params,
             name=f"stage{n}",
-        )(scal, co, *state[:3], *exchange(*state[3:]), *extra)
+        )(co, *state[:5], *exchange(*state[5:]), *extra)
     return tuple(s.reshape(magnetic.shape) for s in state)
 
 

time: 66.2 us -> 48.4 us (0.73)
  Pallas kernels: 31.7 us -> 17.6 us
  local copies, waits for them, and re-layouts: 3.77 us -> 1.92 us
  other arithmetic: 1.22 us -> 0 us
  waiting for transfers between devices: 7.41 us -> 6.74 us
    pallas_call x4, Pallas kernels: 31.7 us -> 17.6 us  [the longest x3 16.8 us: body(): pl.pallas_call(functools.partial(stage_kernel, z, weight, last), out_shap...]
    unnamed x32 -> x4, local copies, waits for them, and re-layouts: 2.82 us -> 1.92 us
    broadcast_in_dim x2 -> x0, local copies, waits for them, and re-layouts: 0.78 us -> none  [the longest x1 0.71 us: body(): co = jnp.broadcast_to(table[:, None], (z.k_n, L))]
    ppermute x3, waiting for transfers between devices: 7.38 us -> 6.71 us  [exchange(): p = lax.ppermute(p, 'phi', left)]
where the time goes in v2:
time: 48.4 us; the launch traced here: 48.2 us
  starting transfers between devices  21.2 us (44%)
  Pallas kernels  17.6 us (36%)
  waiting for transfers between devices  6.74 us (14%)
  local copies, waits for them, and re-layouts  1.92 us (4%)
  between operations  0.75 us (2%)
    pallas_call x3, Pallas kernels, body(): pl.pallas_call(functools.partial(stage_kernel, z, weight, last), out_shap...  16.8 us
    ppermute x3, starting transfers between devices, exchange(): lax.ppermute(rb, 'row', row_b)  12.3 us
    ppermute x3, waiting for transfers between devices, exchange(): p = lax.ppermute(p, 'phi', left)  6.71 us
    ppermute x3, starting transfers between devices, exchange(): lax.ppermute(tb, ('theta', 'phi'), polar_pairs(0))  3.06 us
    ppermute x3, starting transfers between devices, exchange(): lax.ppermute(ta, ('theta', 'phi'), polar_pairs(1))  2.9 us
    ppermute x3, starting transfers between devices, exchange(): p = lax.ppermute(p, 'phi', left)  2.66 us
    unnamed x4, local copies, waits for them, and re-layouts  1.92 us
  transfers between devices with their start and end apart: 15, of which 3 were waited for; matrix products, arithmetic and copies ran while one was open for 0% of the time, Pallas kernels for 0%

profile of v2, /device:TPU:1, one launch (start us, length us, event | category | flops | bytes accessed | tf_op | source)
XLA Modules:
  0.0 48.2 jit_solution(14510701621186230486)
XLA Ops:
  0.6 0.0 copy-start
  0.6 1.0 %copy-done = f32[3,12,16,128]{3,2,1,0:T(8,128)S(1)} copy-done((f32[3,12,16,128]{3,2,1,0:T(8,128)S(1)}, f32[3,12,16,128]{3,2,1,0:T(8,128)}, u32[]{:S(2)}) %copy-start) | copy-done | bytes 294936
  1.6 0.0 copy-start.1
  1.6 1.0 %copy-done.1 = f32[3,12,16,128]{3,2,1,0:T(8,128)S(1)} copy-done((f32[3,12,16,128]{3,2,1,0:T(8,128)S(1)}, f32[3,12,16,128]{3,2,1,0:T(8,128)}, u32[]{:S(2)}) %copy-start.1) | copy-done | bytes 294936
  2.6 0.8 %first.1 = (f32[184,128]{1,0:T(8,128)S(1)}, f32[1152,128]{1,0:T(8,128)S(1)}, f32[768,128]{1,0:T(8,128)S(1)}, f32[1152,128]{1,0:T(8,128)S(1)}, f32[768,128]{1,0:T...) custom-call(f32[576,128]{1,0:T(8,128)S(1)} %bitcast.4, ...), custom_call_target="tpu_custom_call" | custom-call | tf_op jit(solution)/shard_map/first/pallas_call | solution.py:507
  3.3 0.1 collective-permute-start
  3.4 4.5 %collective-permute-start.1 = (f32[288,128]{1,0:T(8,128)S(1)}, f32[288,128]{1,0:T(8,128)S(1)}, u32[]{:S(2)}, u32[]{:S(2)}) collective-permute-start(f32[288,128]{1,0:T(8,128)S(1)} %get-tuple-element.42), channel_id=1, source_target_pairs={{8,16},{16,8},{9,17},{17,9},{10,18},{18,10},{11,19},{19,11},{12,20... | collective-permute-start | bytes 442376 | tf_op jit(solution)/shard_map/ppermute | solution.py:501
  7.9 1.3 %collective-permute-start.2 = (f32[216,128]{1,0:T(8,128)S(1)}, f32[216,128]{1,0:T(8,128)S(1)}, u32[]{:S(2)}, u32[]{:S(2)}) collective-permute-start(f32[216,128]{1,0:T(8,128)S(1)} %get-tuple-element.43), channel_id=1, source_target_pairs={{0,1},{1,0},{2,4},{4,2},{3,5},{5,3},{6,7},{7,6},{8,9},{9,8},{10,12... | collective-permute-start | bytes 331784 | tf_op jit(solution)/shard_map/ppermute | solution.py:502
  9.2 1.4 %collective-permute-start.3 = (f32[216,128]{1,0:T(8,128)S(1)}, f32[216,128]{1,0:T(8,128)S(1)}, u32[]{:S(2)}, u32[]{:S(2)}) collective-permute-start(f32[216,128]{1,0:T(8,128)S(1)} %get-tuple-element.44), channel_id=1, source_target_pairs={{0,2},{2,0},{1,3},{3,1},{4,6},{6,4},{5,7},{7,5},{8,10},{10,8},{9,1... | collective-permute-start | bytes 331784 | tf_op jit(solution)/shard_map/ppermute | solution.py:503
  10.6 1.2 %collective-permute-start.4 = (f32[6,15,128]{2,1,0:T(8,128)S(1)}, f32[6,15,128]{2,1,0:T(8,128)S(1)}, u32[]{:S(2)}, u32[]{:S(2)}) collective-permute-start(f32[6,15,128]{2,1,0:T(8,128)S(1)} %get-tuple-element.45), channel_id=1, source_target_pairs={{0,1},{1,0},{2,3},{3,2},{4,5},{5,4},{6,7},{7,6},{8,9},{9,8},{10,11... | collective-permute-start | bytes 138248 | tf_op jit(solution)/shard_map/ppermute | solution.py:494
  11.8 1.7 %collective-permute-done.4.refs_10_ = f32[6,15,128]{2,1,0:T(8,128)S(1)} collective-permute-done((f32[6,15,128]{2,1,0:T(8,128)S(1)}, f32[6,15,128]{2,1,0:T(8,128)S(1)}, u32[]{:S(2)}, u32[]{:S(2)}) %collective-permute-start.4) | collective-permute-done | bytes 46112 | tf_op jit(solution)/shard_map/ppermute | solution.py:494
  13.5 0.0 collective-permute-done.2.refs_8_
  13.5 0.0 collective-permute-done.3.refs_9_
  13.5 0.0 collective-permute-done.refs_6_
  13.5 0.0 collective-permute-done.1.refs_7_
  13.5 5.5 %stage0.1 = (f32[1152,128]{1,0:T(8,128)S(1)}, f32[768,128]{1,0:T(8,128)S(1)}, f32[1152,128]{1,0:T(8,128)S(1)}, f32[768,128]{1,0:T(8,128)S(1)}, f32[15,128,128]{2...) custom-call(f32[184,128]{1,0:T(8,128)S(1)} %get-tuple-element.35.ref, ...), custom_call_target="tpu_custom_call" | custom-call | tf_op jit(solution)/shard_map/stage0/pallas_call | solution.py:521
  19.1 0.1 collective-permute-start.5
  19.1 4.2 %collective-permute-start.6 = (f32[288,128]{1,0:T(8,128)S(1)}, f32[288,128]{1,0:T(8,128)S(1)}, u32[]{:S(2)}, u32[]{:S(2)}) collective-permute-start(f32[288,128]{1,0:T(8,128)S(1)} %get-tuple-element.52), channel_id=1, source_target_pairs={{8,16},{16,8},{9,17},{17,9},{10,18},{18,10},{11,19},{19,11},{12,20... | collective-permute-start | bytes 442376 | tf_op jit(solution)/shard_map/ppermute | solution.py:501
  23.4 1.3 %collective-permute-start.7 = (f32[216,128]{1,0:T(8,128)S(1)}, f32[216,128]{1,0:T(8,128)S(1)}, u32[]{:S(2)}, u32[]{:S(2)}) collective-permute-start(f32[216,128]{1,0:T(8,128)S(1)} %get-tuple-element.53), channel_id=1, source_target_pairs={{0,1},{1,0},{2,4},{4,2},{3,5},{5,3},{6,7},{7,6},{8,9},{9,8},{10,12... | collective-permute-start | bytes 331784 | tf_op jit(solution)/shard_map/ppermute | solution.py:502
  24.7 1.3 %collective-permute-start.8 = (f32[216,128]{1,0:T(8,128)S(1)}, f32[216,128]{1,0:T(8,128)S(1)}, u32[]{:S(2)}, u32[]{:S(2)}) collective-permute-start(f32[216,128]{1,0:T(8,128)S(1)} %get-tuple-element.54), channel_id=1, source_target_pairs={{0,2},{2,0},{1,3},{3,1},{4,6},{6,4},{5,7},{7,5},{8,10},{10,8},{9,1... | collective-permute-start | bytes 331784 | tf_op jit(solution)/shard_map/ppermute | solution.py:503
  26.0 0.2 collective-permute-start.9
  26.2 2.7 %collective-permute-done.9.refs_10_ = f32[6,15,128]{2,1,0:T(8,128)S(1)} collective-permute-done((f32[6,15,128]{2,1,0:T(8,128)S(1)}, f32[6,15,128]{2,1,0:T(8,128)S(1)}, u32[]{:S(2)}, u32[]{:S(2)}) %collective-permute-start.9) | collective-permute-done | bytes 46112 | tf_op jit(solution)/shard_map/ppermute | solution.py:494
  28.9 0.0 collective-permute-done.7.refs_8_
  28.9 0.0 collective-permute-done.8.refs_9_
  28.9 0.0 collective-permute-done.5.refs_6_
  28.9 0.0 collective-permute-done.6.refs_7_
  28.9 5.6 %stage1.1 = (f32[1152,128]{1,0:T(8,128)S(1)}, f32[768,128]{1,0:T(8,128)S(1)}, f32[1152,128]{1,0:T(8,128)S(1)}, f32[768,128]{1,0:T(8,128)S(1)}, f32[15,128,128]{2...) custom-call(f32[184,128]{1,0:T(8,128)S(1)} %get-tuple-element.35.ref, ...), custom_call_target="tpu_custom_call" | custom-call | tf_op jit(solution)/shard_map/stage1/pallas_call | solution.py:521
  34.5 0.1 collective-permute-start.10
  34.6 3.6 %collective-permute-start.11 = (f32[288,128]{1,0:T(8,128)S(1)}, f32[288,128]{1,0:T(8,128)S(1)}, u32[]{:S(2)}, u32[]{:S(2)}) collective-permute-start(f32[288,128]{1,0:T(8,128)S(1)} %get-tuple-element.62), channel_id=1, source_target_pairs={{8,16},{16,8},{9,17},{17,9},{10,18},{18,10},{11,19},{19,11},{12,20... | collective-permute-start | bytes 442376 | tf_op jit(solution)/shard_map/ppermute | solution.py:501
  38.2 0.3 collective-permute-start.12
  38.5 0.4 collective-permute-start.13
  39.0 1.2 %collective-permute-start.14 = (f32[6,15,128]{2,1,0:T(8,128)S(1)}, f32[6,15,128]{2,1,0:T(8,128)S(1)}, u32[]{:S(2)}, u32[]{:S(2)}) collective-permute-start(f32[6,15,128]{2,1,0:T(8,128)S(1)} %get-tuple-element.65), channel_id=1, source_target_pairs={{0,1},{1,0},{2,3},{3,2},{4,5},{5,4},{6,7},{7,6},{8,9},{9,8},{10,11... | collective-permute-start | bytes 138248 | tf_op jit(solution)/shard_map/ppermute | solution.py:494
  40.1 2.3 %collective-permute-done.14.refs_10_ = f32[6,15,128]{2,1,0:T(8,128)S(1)} collective-permute-done((f32[6,15,128]{2,1,0:T(8,128)S(1)}, f32[6,15,128]{2,1,0:T(8,128)S(1)}, u32[]{:S(2)}, u32[]{:S(2)}) %collective-permute-start.14) | collective-permute-done | bytes 46112 | tf_op jit(solution)/shard_map/ppermute | solution.py:494
  42.4 0.0 collective-permute-done.12.refs_8_
  42.4 0.0 collective-permute-done.13.refs_9_
  42.4 0.0 collective-permute-done.10.refs_6_
  42.5 0.0 collective-permute-done.11.refs_7_
  42.5 5.7 %stage2.1 = (f32[576,128]{1,0:T(8,128)}, f32[576,128]{1,0:T(8,128)}) custom-call(f32[184,128]{1,0:T(8,128)S(1)} %get-tuple-element.35.refs_0_, f32[1152,128]{1,0:T(8,128)S(1)} %get-tuple-element.56.refs_1_, f32[768,128]{1,0:T(8,128)S(1)} %get-tuple-element.57.refs_2_, f32[1152,128]{1,0:T(8,128)S(1)} %get-tuple-element.58.refs_3_, ...), custom_call_target="tpu_custom_call" | custom-call | tf_op jit(solution)/shard_map/stage2/pallas_call | solution.py:521
Async XLA Ops:
  0.6 1.0 %copy-start = (f32[3,12,16,128]{3,2,1,0:T(8,128)S(1)}, f32[3,12,16,128]{3,2,1,0:T(8,128)}, u32[]{:S(2)}) copy-start(f32[3,12,16,128]{3,2,1,0:T(8,128)} %param.2) | copy-start | bytes 884740
  1.6 1.0 %copy-start.1 = (f32[3,12,16,128]{3,2,1,0:T(8,128)S(1)}, f32[3,12,16,128]{3,2,1,0:T(8,128)}, u32[]{:S(2)}) copy-start(f32[3,12,16,128]{3,2,1,0:T(8,128)} %param.3) | copy-start | bytes 884740
  3.3 10.2 %collective-permute-start = (f32[288,128]{1,0:T(8,128)S(1)}, f32[288,128]{1,0:T(8,128)S(1)}, u32[]{:S(2)}, u32[]{:S(2)}) collective-permute-start(f32[288,128]{1,0:T(8,128)S(1)} %get-tuple-element.41), channel_id=1, source_target_pairs={{0,8},{8,0},{16,24},{24,16},{1,9},{9,1},{17,25},{25,17},{2,10},{10... | collective-permute-start | bytes 442376 | tf_op jit(solution)/shard_map/ppermute | solution.py:500
  3.4 10.1 %collective-permute-start.1 = (f32[288,128]{1,0:T(8,128)S(1)}, f32[288,128]{1,0:T(8,128)S(1)}, u32[]{:S(2)}, u32[]{:S(2)}) collective-permute-start(f32[288,128]{1,0:T(8,128)S(1)} %get-tuple-element.42), channel_id=1, source_target_pairs={{8,16},{16,8},{9,17},{17,9},{10,18},{18,10},{11,19},{19,11},{12,20... | collective-permute-start | bytes 442376 | tf_op jit(solution)/shard_map/ppermute | solution.py:501
  7.9 5.6 %collective-permute-start.2 = (f32[216,128]{1,0:T(8,128)S(1)}, f32[216,128]{1,0:T(8,128)S(1)}, u32[]{:S(2)}, u32[]{:S(2)}) collective-permute-start(f32[216,128]{1,0:T(8,128)S(1)} %get-tuple-element.43), channel_id=1, source_target_pairs={{0,1},{1,0},{2,4},{4,2},{3,5},{5,3},{6,7},{7,6},{8,9},{9,8},{10,12... | collective-permute-start | bytes 331784 | tf_op jit(solution)/shard_map/ppermute | solution.py:502
  9.2 4.3 %collective-permute-start.3 = (f32[216,128]{1,0:T(8,128)S(1)}, f32[216,128]{1,0:T(8,128)S(1)}, u32[]{:S(2)}, u32[]{:S(2)}) collective-permute-start(f32[216,128]{1,0:T(8,128)S(1)} %get-tuple-element.44), channel_id=1, source_target_pairs={{0,2},{2,0},{1,3},{3,1},{4,6},{6,4},{5,7},{7,5},{8,10},{10,8},{9,1... | collective-permute-start | bytes 331784 | tf_op jit(solution)/shard_map/ppermute | solution.py:503
  10.6 2.9 %collective-permute-start.4 = (f32[6,15,128]{2,1,0:T(8,128)S(1)}, f32[6,15,128]{2,1,0:T(8,128)S(1)}, u32[]{:S(2)}, u32[]{:S(2)}) collective-permute-start(f32[6,15,128]{2,1,0:T(8,128)S(1)} %get-tuple-element.45), channel_id=1, source_target_pairs={{0,1},{1,0},{2,3},{3,2},{4,5},{5,4},{6,7},{7,6},{8,9},{9,8},{10,11... | collective-permute-start | bytes 138248 | tf_op jit(solution)/shard_map/ppermute | solution.py:494
  19.1 9.9 %collective-permute-start.5 = (f32[288,128]{1,0:T(8,128)S(1)}, f32[288,128]{1,0:T(8,128)S(1)}, u32[]{:S(2)}, u32[]{:S(2)}) collective-permute-start(f32[288,128]{1,0:T(8,128)S(1)} %get-tuple-element.51), channel_id=1, source_target_pairs={{0,8},{8,0},{16,24},{24,16},{1,9},{9,1},{17,25},{25,17},{2,10},{10... | collective-permute-start | bytes 442376 | tf_op jit(solution)/shard_map/ppermute | solution.py:500
  19.1 9.8 %collective-permute-start.6 = (f32[288,128]{1,0:T(8,128)S(1)}, f32[288,128]{1,0:T(8,128)S(1)}, u32[]{:S(2)}, u32[]{:S(2)}) collective-permute-start(f32[288,128]{1,0:T(8,128)S(1)} %get-tuple-element.52), channel_id=1, source_target_pairs={{8,16},{16,8},{9,17},{17,9},{10,18},{18,10},{11,19},{19,11},{12,20... | collective-permute-start | bytes 442376 | tf_op jit(solution)/shard_map/ppermute | solution.py:501
  23.4 5.5 %collective-permute-start.7 = (f32[216,128]{1,0:T(8,128)S(1)}, f32[216,128]{1,0:T(8,128)S(1)}, u32[]{:S(2)}, u32[]{:S(2)}) collective-permute-start(f32[216,128]{1,0:T(8,128)S(1)} %get-tuple-element.53), channel_id=1, source_target_pairs={{0,1},{1,0},{2,4},{4,2},{3,5},{5,3},{6,7},{7,6},{8,9},{9,8},{10,12... | collective-permute-start | bytes 331784 | tf_op jit(solution)/shard_map/ppermute | solution.py:502
  24.7 4.2 %collective-permute-start.8 = (f32[216,128]{1,0:T(8,128)S(1)}, f32[216,128]{1,0:T(8,128)S(1)}, u32[]{:S(2)}, u32[]{:S(2)}) collective-permute-start(f32[216,128]{1,0:T(8,128)S(1)} %get-tuple-element.54), channel_id=1, source_target_pairs={{0,2},{2,0},{1,3},{3,1},{4,6},{6,4},{5,7},{7,5},{8,10},{10,8},{9,1... | collective-permute-start | bytes 331784 | tf_op jit(solution)/shard_map/ppermute | solution.py:503
  26.0 2.9 %collective-permute-start.9 = (f32[6,15,128]{2,1,0:T(8,128)S(1)}, f32[6,15,128]{2,1,0:T(8,128)S(1)}, u32[]{:S(2)}, u32[]{:S(2)}) collective-permute-start(f32[6,15,128]{2,1,0:T(8,128)S(1)} %get-tuple-element.55), channel_id=1, source_target_pairs={{0,1},{1,0},{2,3},{3,2},{4,5},{5,4},{6,7},{7,6},{8,9},{9,8},{10,11... | collective-permute-start | bytes 138248 | tf_op jit(solution)/shard_map/ppermute | solution.py:494
  34.5 7.9 %collective-permute-start.10 = (f32[288,128]{1,0:T(8,128)S(1)}, f32[288,128]{1,0:T(8,128)S(1)}, u32[]{:S(2)}, u32[]{:S(2)}) collective-permute-start(f32[288,128]{1,0:T(8,128)S(1)} %get-tuple-element.61), channel_id=1, source_target_pairs={{0,8},{8,0},{16,24},{24,16},{1,9},{9,1},{17,25},{25,17},{2,10},{10... | collective-permute-start | bytes 442376 | tf_op jit(solution)/shard_map/ppermute | solution.py:500
  34.6 7.8 %collective-permute-start.11 = (f32[288,128]{1,0:T(8,128)S(1)}, f32[288,128]{1,0:T(8,128)S(1)}, u32[]{:S(2)}, u32[]{:S(2)}) collective-permute-start(f32[288,128]{1,0:T(8,128)S(1)} %get-tuple-element.62), channel_id=1, source_target_pairs={{8,16},{16,8},{9,17},{17,9},{10,18},{18,10},{11,19},{19,11},{12,20... | collective-permute-start | bytes 442376 | tf_op jit(solution)/shard_map/ppermute | solution.py:501
  38.2 4.2 %collective-permute-start.12 = (f32[216,128]{1,0:T(8,128)S(1)}, f32[216,128]{1,0:T(8,128)S(1)}, u32[]{:S(2)}, u32[]{:S(2)}) collective-permute-start(f32[216,128]{1,0:T(8,128)S(1)} %get-tuple-element.63), channel_id=1, source_target_pairs={{0,1},{1,0},{2,4},{4,2},{3,5},{5,3},{6,7},{7,6},{8,9},{9,8},{10,12... | collective-permute-start | bytes 331784 | tf_op jit(solution)/shard_map/ppermute | solution.py:502
  38.5 3.9 %collective-permute-start.13 = (f32[216,128]{1,0:T(8,128)S(1)}, f32[216,128]{1,0:T(8,128)S(1)}, u32[]{:S(2)}, u32[]{:S(2)}) collective-permute-start(f32[216,128]{1,0:T(8,128)S(1)} %get-tuple-element.64), channel_id=1, source_target_pairs={{0,2},{2,0},{1,3},{3,1},{4,6},{6,4},{5,7},{7,5},{8,10},{10,8},{9,1... | collective-permute-start | bytes 331784 | tf_op jit(solution)/shard_map/ppermute | solution.py:503
  39.0 3.5 %collective-permute-start.14 = (f32[6,15,128]{2,1,0:T(8,128)S(1)}, f32[6,15,128]{2,1,0:T(8,128)S(1)}, u32[]{:S(2)}, u32[]{:S(2)}) collective-permute-start(f32[6,15,128]{2,1,0:T(8,128)S(1)} %get-tuple-element.65), channel_id=1, source_target_pairs={{0,1},{1,0},{2,3},{3,2},{4,5},{5,4},{6,7},{7,6},{8,9},{9,8},{10,11... | collective-permute-start | bytes 138248 | tf_op jit(solution)/shard_map/ppermute | solution.py:494
